TPU v7x, 8 devices: a whole 2x2x1 slice. The times are simulated.
8 devices in a mesh: rep: 2 (over z, y), rows: 4 (over x, core).
Axes of the slice: x: 2, y: 2, z: 1, core: 2. Of those that a mesh axis runs over, the one named last changes fastest.
Arguments:
- adjacency: bfloat16 [8192, 8192], P('rows', 'rep')
- features: bfloat16 [8192, 100], P('rows')
- w_one: bfloat16 [100, 256], replicated
- w_two: bfloat16 [256, 47], replicated
- grad_out: float32 [8192, 47], P('rows')
Outputs:
- output 1: float32 [100, 256], replicated
- output 2: float32 [256, 47], replicated
All inputs are finite; a program needn't handle non-finite values.
Results may differ from a plain program's by a relative error of at most 0.001.
Values are sent between devices in bfloat16 or wider.
A program may use at most 1 GiB of HBM per device.

v0:
```python
import jax
import jax.numpy as jnp
from jax import lax
from jax.sharding import PartitionSpec as P

ROWS_DIMS = (((0,), (0,)), ((), ()))
COLS_DIMS = (((1,), (1,)), ((), ()))


def solution(mesh):
    row_count = mesh.shape["rows"]
    rep_count = mesh.shape["rep"]
    both_axes = ("rep", "rows")
    to_ranges = [(rep_pos * row_count + row_pos, row_pos * rep_count + rep_pos) for rep_pos in range(rep_count) for row_pos in range(row_count)]
    to_blocks = [(dst_dev, src_dev) for src_dev, dst_dev in to_ranges]

    def column_rows(node_block, rep_pos):
        piece_rows = node_block.shape[0] // rep_count
        own_part = lax.dynamic_slice_in_dim(node_block, rep_pos * piece_rows, piece_rows, axis=0)
        arrived = lax.ppermute(own_part, both_axes, perm=to_ranges)
        return lax.all_gather(arrived, "rows", axis=0, tiled=True)

    def local_step(adj_blk, feat_blk, w_one, w_two, grad_blk):
        rep_pos = lax.axis_index("rep")
        piece_rows = feat_blk.shape[0] // rep_count
        row_start = rep_pos * piece_rows
        feat_range = column_rows(feat_blk, rep_pos)
        agg_one = lax.psum(jnp.dot(adj_blk, feat_range, preferred_element_type=jnp.float32), "rep")
        act_one = agg_one.astype(jnp.bfloat16)
        hidden = jnp.maximum(jnp.dot(act_one, w_one, preferred_element_type=jnp.float32), 0.0).astype(jnp.bfloat16)
        hidden_range = column_rows(hidden, rep_pos)
        agg_two = lax.psum(jnp.dot(adj_blk, hidden_range, preferred_element_type=jnp.float32), "rep")
        act_two = agg_two.astype(jnp.bfloat16)
        grad_b = grad_blk.astype(jnp.bfloat16)
        act_two_part = lax.dynamic_slice_in_dim(act_two, row_start, piece_rows, axis=0)
        grad_part = lax.dynamic_slice_in_dim(grad_b, row_start, piece_rows, axis=0)
        dw_two = lax.dot_general(act_two_part, grad_part, ROWS_DIMS, preferred_element_type=jnp.float32)
        d_agg = lax.dot_general(grad_b, w_two, COLS_DIMS, preferred_element_type=jnp.float32).astype(jnp.bfloat16)
        d_partial = lax.dot_general(adj_blk, d_agg, ROWS_DIMS, preferred_element_type=jnp.float32)
        d_piece = lax.psum_scatter(d_partial, "rows", scatter_dimension=0, tiled=True)
        d_hidden = lax.ppermute(d_piece, both_axes, perm=to_blocks)
        hidden_part = lax.dynamic_slice_in_dim(hidden, row_start, piece_rows, axis=0)
        act_one_part = lax.dynamic_slice_in_dim(act_one, row_start, piece_rows, axis=0)
        d_pre = jnp.where(hidden_part > 0, d_hidden, 0.0).astype(jnp.bfloat16)
        dw_one = lax.dot_general(act_one_part, d_pre, ROWS_DIMS, preferred_element_type=jnp.float32)
        return lax.psum(dw_one, both_axes), lax.psum(dw_two, both_axes)

    return jax.shard_map(local_step, mesh=mesh, in_specs=(P("rows", "rep"), P("rows", None), P(), P(), P("rows", None)), out_specs=(P(), P()), check_vma=False)
```

profile of v0, /device:TPU:0, one launch (start us, length us, event | category | flops | bytes accessed | tf_op | source)
XLA Modules:
  0.0 264.5 jit_solution(7964022396420630494)
XLA Ops:
  7.2 0.0 copy-start
  7.2 0.0 copy-start.3
  7.2 0.0 copy-start.2
  7.2 0.0 all-gather.2.cloned.1.call-start
  7.3 0.9 copy-done
  8.2 0.7 collective-permute-start
  8.9 0.0 collective-permute-done
  8.9 20.9 %all_gather.6 = bf16[4096,100]{0,1:T(8,128)(2,1)S(1)} all-gather(bf16[1024,100]{0,1:T(8,128)(2,1)S(1)} %collective-permute-done), channel_id=1, replica_groups=mesh['rep'=2,'rows'=4] {'rows'}, dimensions={0}, use_global_device_ids=true | all-gather | bytes 1024000 | tf_op jit(solution)/shard_map/all_gather | solution.py:21
  29.8 11.0 %convolution_bitcast_fusion.2 = f32[2048,100]{0,1:T(8,128)S(1)} fusion(bf16[4096,100]{0,1:T(8,128)(2,1)S(1)} %all_gather.6, bf16[2048,4096]{1,0:T(8,128)(2,1)} %param.5), kind=kOutput, calls=%fused_computation.3 | convolution fusion | flops 1677721600 | bytes 18415616 | tf_op jit(solution)/shard_map/dot_general | solution.py:28
  40.8 24.3 %all-reduce.5 = bf16[2048,100]{0,1:T(8,128)(2,1)S(1)} all-reduce(f32[2048,100]{0,1:T(8,128)S(1)} %convolution_bitcast_fusion.2), channel_id=1, replica_groups=mesh['rep'=2,'rows'=4] {'rep'}, use_global_device_ids=true, to_apply=%region_0.0 | all-reduce | flops 204800 | bytes 1228800 | tf_op jit(solution)/shard_map/psum | solution.py:28
  65.1 0.5 fusion.12
  65.6 0.1 fusion
  65.7 0.7 collective-permute-start.2
  66.4 0.0 collective-permute-done.2
  66.4 0.8 copy-done.1
  67.2 0.0 all-gather.2.cloned.1.call-update
  67.2 0.0 reduce-scatter.2.cloned.1.call-start
  67.3 12.0 %convolution_bitcast_fusion = f32[4096,256]{1,0:T(8,128)} fusion(bf16[2048,4096]{1,0:T(8,128)(2,1)} %param.5, bf16[2048,47]{0,1:T(8,128)(2,1)S(1)} %convert_element_type.20, bf16[256,47]{0,1:T(8,128)(2,1)S(1)} %copy-done.4), kind=kOutput, calls=%fused_computation | convolution fusion | flops 4344774656 | bytes 21188096 | tf_op jit(solution)/shard_map/dot_general | solution.py:39
  79.4 0.0 reduce-scatter.2.cloned.1.call-update
  79.4 0.2 all-reduce.4.cloned.1.call-start
  79.6 18.0 %all-gather.2.cloned.1.call-done = bf16[4096,256]{1,0:T(8,128)(2,1)} async-done(((bf16[1024,256]{1,0:T(8,128)(2,1)}), bf16[4096,256]{1,0:T(8,128)(2,1)}) %all-gather.2.cloned.1.call-update) | async-done | bytes 2097168 | tf_op jit(solution)/shard_map/all_gather | solution.py:21
  97.6 12.3 %convolution_bitcast_fusion.1 = f32[2048,256]{0,1:T(8,128)} fusion(bf16[4096,256]{1,0:T(8,128)(2,1)} %all-gather.2.cloned.1.call-done, bf16[2048,4096]{1,0:T(8,128)(2,1)} %param.5), kind=kOutput, calls=%fused_computation.1 | convolution fusion | flops 4294967296 | bytes 20971520 | tf_op jit(solution)/shard_map/dot_general | solution.py:32
  109.9 28.5 %reduce-scatter.2.cloned.1.call-done = f32[1024,256]{1,0:T(8,128)} async-done(((f32[4096,256]{1,0:T(8,128)}), f32[1024,256]{1,0:T(8,128)}) %reduce-scatter.2.cloned.1.call-update) | async-done | bytes 1048592 | tf_op jit(solution)/shard_map/reduce_scatter | solution.py:40
  138.4 9.5 %collective-permute-start.1 = (f32[1024,256]{1,0:T(8,128)}, f32[1024,256]{1,0:T(8,128)}, u32[]{:S(2)}, u32[]{:S(2)}) collective-permute-start(f32[1024,256]{1,0:T(8,128)} %reduce-scatter.2.cloned.1.call-done), channel_id=1, source_target_pairs={{0,0},{2,1},{4,2},{6,3},{1,4},{3,5},{5,6},{7,7}} | collective-permute-start | bytes 3145736 | tf_op jit(solution)/shard_map/ppermute | solution.py:41
  147.9 57.7 %all-reduce.6 = bf16[2048,256]{0,1:T(8,128)(2,1)S(1)} all-reduce(f32[2048,256]{0,1:T(8,128)} %convolution_bitcast_fusion.1), channel_id=1, replica_groups=mesh['rep'=2,'rows'=4] {'rep'}, use_global_device_ids=true, to_apply=%region_3.4 | all-reduce | flops 524288 | bytes 3145728 | tf_op jit(solution)/shard_map/psum | solution.py:32
  205.6 0.0 collective-permute-done.1
  205.6 2.2 fusion.1
  207.7 0.0 all-reduce.4.cloned.1.call-update
  207.8 0.3 fusion.2
  208.0 29.3 %psum.31 = f32[256,47]{0,1:T(8,128)} all-reduce(f32[256,47]{0,1:T(8,128)S(1)} %fusion.2), channel_id=1, replica_groups=mesh['rep'=2,'rows'=4] {'rep','rows'}, use_global_device_ids=true, to_apply=%region_4.5 | all-reduce | flops 12032 | bytes 96256 | tf_op jit(solution)/shard_map/psum | solution.py:46
  237.4 19.0 %all-reduce.4.cloned.1.call-done = f32[100,256]{1,0:T(8,128)} async-done(((f32[100,256]{1,0:T(8,128)}), f32[100,256]{1,0:T(8,128)}) %all-reduce.4.cloned.1.call-update) | async-done | bytes 102416 | tf_op jit(solution)/shard_map/psum | solution.py:46
  256.4 1.5 copy.12
  (7 shorter events, 0.0 us)
Async XLA Ops:
  7.2 1.0 copy-start
  7.2 57.9 %copy-start.3 = (bf16[100,256]{1,0:T(8,128)(2,1)S(1)}, bf16[100,256]{1,0:T(8,128)(2,1)}, u32[]{:S(2)}) copy-start(bf16[100,256]{1,0:T(8,128)(2,1)} %param.7) | copy-start | bytes 153604
  7.2 60.1 %copy-start.2 = (f32[2048,47]{0,1:T(8,128)S(1)}, f32[2048,47]{0,1:T(8,128)}, u32[]{:S(2)}) copy-start(f32[2048,47]{0,1:T(8,128)} %param.9) | copy-start | bytes 1155076
  7.2 60.1 %copy-start.4 = (bf16[256,47]{0,1:T(8,128)(2,1)S(1)}, bf16[256,47]{0,1:T(8,128)(2,1)}, u32[]{:S(2)}) copy-start(bf16[256,47]{0,1:T(8,128)(2,1)} %param.8) | copy-start | bytes 72196
  7.2 90.4 %all-gather.2.cloned.1.call-start = ((), (), s32[]{:S(2)}) async-start(), calls=%async_computation.3 | async-start | bytes 2621440 | tf_op jit(solution)/shard_map/all_gather | solution.py:21
  8.2 0.7 collective-permute-start
  65.7 0.7 collective-permute-start.2
  66.4 0.8 copy-start.1
  67.2 71.2 %reduce-scatter.2.cloned.1.call-start = ((), (), s32[]{:S(2)}) async-start(), calls=%async_computation.1 | async-start | bytes 5242880 | tf_op jit(solution)/shard_map/reduce_scatter | solution.py:40
  79.4 177.0 %all-reduce.4.cloned.1.call-start = ((), (), s32[]{:S(2)}) async-start(), calls=%async_computation.2 | async-start | bytes 212992 | tf_op jit(solution)/shard_map/psum | solution.py:46
  138.4 67.2 %collective-permute-start.1 = (f32[1024,256]{1,0:T(8,128)}, f32[1024,256]{1,0:T(8,128)}, u32[]{:S(2)}, u32[]{:S(2)}) collective-permute-start(f32[1024,256]{1,0:T(8,128)} %reduce-scatter.2.cloned.1.call-done), channel_id=1, source_target_pairs={{0,0},{2,1},{4,2},{6,3},{1,4},{3,5},{5,6},{7,7}} | collective-permute-start | bytes 3145736 | tf_op jit(solution)/shard_map/ppermute | solution.py:41
Sparse Core Ops, SparseCore 0:
  67.4 30.2 all-gather.1
  100.1 38.2 reduce-scatter.1
  207.9 48.5 all-reduce.3
where the time goes:
time: 265 us
  blocking collectives  132 us (50%)
  waiting for transfers between devices  65.6 us (25%)
  matrix products  38.3 us (14%)
  between operations  13.9 us (5%)
  starting transfers between devices  11.1 us (4%)
  local copies, waits for them, and re-layouts  3.29 us (1%)
    psum x1, blocking collectives, local_step(): lax.psum(jnp.dot(adj_blk, hidden_range, preferred_element_type=jnp.float3...  57.7 us
    psum x1, blocking collectives, local_step(): return (lax.psum(dw_one, both_axes), lax.psum(dw_two, both_axes))  29.3 us
    reduce_scatter x1, waiting for transfers between devices, local_step(): lax.psum_scatter(d_partial, 'rows', scatter_dimension=0, tiled=True)  28.5 us
    psum x1, blocking collectives, local_step(): lax.psum(jnp.dot(adj_blk, feat_range, preferred_element_type=jnp.float32)...  24.3 us
    all_gather x1, blocking collectives, column_rows(): return lax.all_gather(arrived, 'rows', axis=0, tiled=True)  20.9 us
    psum x1, waiting for transfers between devices, local_step(): return (lax.psum(dw_one, both_axes), lax.psum(dw_two, both_axes))  19 us
    all_gather x1, waiting for transfers between devices, column_rows(): return lax.all_gather(arrived, 'rows', axis=0, tiled=True)  18 us
    dot_general x1, matrix products, local_step(): jnp.dot(adj_blk, hidden_range, preferred_element_type=jnp.float32)  12.3 us
  transfers between devices with their start and end apart: 6, of which 3 were waited for; matrix products, arithmetic and copies ran while one was open for 9% of the time, Pallas kernels for 0%

commit v1 on v0

v1 whole, which is shorter than its diff:
```python
import jax
import jax.numpy as jnp
from jax import lax
from jax.experimental import pallas as pl
from jax.experimental.pallas import tpu as pltpu
from jax.sharding import PartitionSpec as P

MESH = pl.DeviceIdType.MESH
F32 = jnp.float32
BF16 = jnp.bfloat16
NN = (((1,), (0,)), ((), ()))
NT = (((1,), (1,)), ((), ()))
TN = (((0,), (0,)), ((), ()))

H_NEAR, H_FAR, HT_D2D, X1_Y, X1_NEAR, X1_FAR, X1_FAR2, X1_D2D = 0, 1, 2, 4, 6, 7, 8, 9
DZ_D2D, DZ_X, X2_Y, AR_ONE, AR_TWO, N_REMOTE = 11, 13, 15, 17, 22, 27
A_CHUNKS = 4


def dot(lhs, rhs, dims):
    return lax.dot_general(lhs, rhs, dims, preferred_element_type=F32)


def ds(start, size, align=128):
    return pl.ds(pl.multiple_of(start, align), size)


def gcn_kernel(
    adj, feat, w_one, w_two, grad, dw1_out, dw2t_out,
    a_v, ht, g_v, w1_v, w2_v, gbt, dyt, dzp, dz_in, dz_s, dz_x,
    x1p, x1_in, x1s, x1t, z1t, x2p, x2_in,
    one_p, one_in, one_all, one_tot, two_p, two_in, two_all, two_tot,
    a_sem, l_sem, send_sem, recv_sem,
):
    y = lax.axis_index("rep")
    r = lax.axis_index("rows")
    x, c = r // 2, lax.rem(r, 2)
    diag = x == y
    peer = (y, 2 * x + 1 - c)
    xn = (y, 2 * (1 - x) + c)
    yn = (1 - y, r)
    opp = (1 - y, 2 * (1 - x) + c)
    rows, cols = a_v.shape
    half, quarter = rows // 2, rows // 4

    def rcopy(src, dst, send, recv, dev):
        return pltpu.make_async_remote_copy(
            src_ref=src, dst_ref=dst, send_sem=send_sem.at[send], recv_sem=recv_sem.at[recv],
            device_id=dev, device_id_type=MESH)

    g_load = pltpu.make_async_copy(grad, g_v, l_sem.at[0])
    w1_load = pltpu.make_async_copy(w_one, w1_v, l_sem.at[1])
    w2_load = pltpu.make_async_copy(w_two, w2_v, l_sem.at[2])
    my_cols, peer_cols = c * rows, (1 - c) * rows
    own_block = ds(my_cols, rows)
    h_load = pltpu.make_async_copy(feat, ht.at[:, own_block], l_sem.at[3])
    g_load.start()
    w1_load.start()
    w2_load.start()

    @pl.when(diag)
    def _():
        h_load.start()

    step = rows // A_CHUNKS
    a_loads = []
    for i in range(A_CHUNKS):
        rng = pl.ds(i * step, step)
        a_loads.append(pltpu.make_async_copy(adj.at[rng], a_v.at[rng], a_sem.at[i]))
        a_loads[-1].start()

    barrier = pltpu.get_barrier_semaphore()
    for dev in (peer, xn, yn, opp):
        pl.semaphore_signal(barrier, inc=1, device_id=dev, device_id_type=MESH)
    pl.semaphore_wait(barrier, 4)

    top, bot = pl.ds(0, half), pl.ds(half, half)
    h_near = rcopy(feat.at[:, top], ht.at[:, ds(my_cols, half)], H_NEAR, H_NEAR, xn)
    h_far = rcopy(feat.at[:, bot], ht.at[:, ds(my_cols + half, half)], H_FAR, H_FAR, opp)

    @pl.when(diag)
    def _():
        h_near.start()

    @pl.when(jnp.logical_not(diag))
    def _():
        h_far.start()

    g_load.wait()
    w2_load.wait()
    gbt[...] = g_v[...].astype(BF16)
    dyt[...] = dot(w2_v[...], gbt[...], TN).astype(BF16)
    for load in a_loads:
        load.wait()

    dz_d2d = []
    for i in range(2):
        cs = ds(peer_cols + i * half, half)
        dzp[:, cs] = dot(dyt[...], a_v[:, cs], NN)
        dz_d2d.append(rcopy(dzp.at[:, cs], dz_in.at[:, pl.ds(i * half, half)], DZ_D2D + i, DZ_D2D + i, peer))
        dz_d2d[-1].start()
    for i in range(2):
        cs = ds(my_cols + i * half, half)
        dzp[:, cs] = dot(dyt[...], a_v[:, cs], NN)

    @pl.when(diag)
    def _():
        h_load.wait()

    @pl.when(jnp.logical_not(diag))
    def _():
        h_near.wait_recv()
        h_far.wait_recv()

    ht_d2d = []
    for i in range(2):
        cs = ds(my_cols + i * half, half)
        ht_d2d.append(rcopy(ht.at[:, cs], ht.at[:, cs], HT_D2D + i, HT_D2D + i, peer))
        ht_d2d[-1].start()
    for copy in ht_d2d:
        copy.wait_recv()

    x1_y = []
    for i in range(2):
        rs = ds((1 - y) * half + i * quarter, quarter)
        x1p[:, rs] = dot(ht[...], a_v[rs, :], NT)
        x1_y.append(rcopy(x1p.at[:, rs], x1_in.at[:, pl.ds(i * quarter, quarter)], X1_Y + i, X1_Y + i, yn))
        x1_y[-1].start()

    dz_d2d[0].wait_recv()
    dz_d2d[1].wait_recv()
    other_x = ds((1 - x) * half, half)
    dz_s[...] = dzp[:, ds(my_cols + (1 - x) * half, half)] + dz_in[:, other_x]
    dz_x_copy = rcopy(dz_s, dz_x, DZ_X, DZ_X, xn)

    for i in range(2):
        rs = ds(y * half + i * quarter, quarter)
        x1p[:, rs] = dot(ht[...], a_v[rs, :], NT)
    for i in range(2):
        x1_y[i].wait_recv()
        rs = ds(y * half + i * quarter, quarter)
        qs = pl.ds(i * quarter, quarter)
        x1s[:, qs] = (x1p[:, rs] + x1_in[:, qs]).astype(BF16)

    slot = ds(c * rows + y * half, half)
    x1_near = rcopy(x1s, x1t.at[:, slot], X1_NEAR, X1_NEAR, xn)
    x1_far = rcopy(x1s, x1t.at[:, slot], X1_FAR, X1_FAR, yn)
    x1_far2 = rcopy(x1s, x1t.at[:, slot], X1_FAR2, X1_FAR, opp)

    @pl.when(diag)
    def _():
        x1_near.start()
        x1t[:, slot] = x1s[...]

    @pl.when(jnp.logical_not(diag))
    def _():
        x1_far2.start()
        x1_far.start()

    dz_x_copy.start()
    w1_load.wait()

    @pl.when(jnp.logical_not(diag))
    def _():
        x1_near.wait_recv()

    near_cols = ds(my_cols + y * half, half)
    far_cols = ds(my_cols + (1 - y) * half, half)
    x1_d2d = [rcopy(x1t.at[:, near_cols], x1t.at[:, near_cols], X1_D2D, X1_D2D, peer),
              rcopy(x1t.at[:, far_cols], x1t.at[:, far_cols], X1_D2D + 1, X1_D2D + 1, peer)]
    x1_d2d[0].start()
    z1t[:, near_cols] = jnp.maximum(dot(w1_v[...], x1t[:, near_cols], TN), 0.0).astype(BF16)
    x1_d2d[0].wait_recv()
    peer_near = ds(peer_cols + y * half, half)
    z1t[:, peer_near] = jnp.maximum(dot(w1_v[...], x1t[:, peer_near], TN), 0.0).astype(BF16)
    x1_far.wait_recv()
    x1_d2d[1].start()
    z1t[:, far_cols] = jnp.maximum(dot(w1_v[...], x1t[:, far_cols], TN), 0.0).astype(BF16)
    x1_d2d[1].wait_recv()
    peer_far = ds(peer_cols + (1 - y) * half, half)
    z1t[:, peer_far] = jnp.maximum(dot(w1_v[...], x1t[:, peer_far], TN), 0.0).astype(BF16)

    x2_y = []
    for i in range(2):
        rs = ds((1 - y) * half + i * quarter, quarter)
        x2p[:, rs] = dot(z1t[...], a_v[rs, :], NT)
        x2_y.append(rcopy(x2p.at[:, rs], x2_in.at[:, pl.ds(i * quarter, quarter)], X2_Y + i, X2_Y + i, yn))
        x2_y[-1].start()
    for i in range(2):
        rs = ds(y * half + i * quarter, quarter)
        x2p[:, rs] = dot(z1t[...], a_v[rs, :], NT)

    def ar_first(part, inn, base):
        n = part.shape[0] // 2
        copy = rcopy(part.at[ds((1 - c) * n, n, 8)], inn, base, base, peer)
        copy.start()
        return copy

    def ar_second(part, inn, alls, base, first):
        n = part.shape[0] // 2
        chip = 2 * x + y
        first.wait_recv()
        alls[chip] = part[ds(c * n, n, 8)] + inn[...]
        copies = []
        for i, dev in enumerate((opp, xn, yn)):
            copies.append(rcopy(alls.at[chip], alls.at[chip], base + 1 + i, base + 1 + i, dev))
            copies[-1].start()
        return copies

    def ar_third(alls, tot, base, second):
        n = alls.shape[1]
        for copy in second:
            copy.wait_recv()
        mine = ds(c * n, n, 8)
        tot[mine] = (alls[0] + alls[1]) + (alls[2] + alls[3])
        copy = rcopy(tot.at[mine], tot.at[mine], base + 4, base + 4, peer)
        copy.start()
        return copy

    own_x = ds(x * half, half)
    dz_cols = ds(my_cols + x * half, half)
    dz_x_copy.wait_recv()
    d_hidden = (dzp[:, dz_cols] + dz_in[:, own_x]) + dz_x[...]
    d_pre = jnp.where(z1t[:, dz_cols].astype(F32) > 0.0, d_hidden, 0.0).astype(BF16)
    feat_in = feat.shape[0]
    one_p[pl.ds(0, feat_in)] = dot(x1t[:, dz_cols], d_pre, NT)
    one_p[pl.ds(feat_in, one_p.shape[0] - feat_in)] = jnp.zeros((one_p.shape[0] - feat_in, one_p.shape[1]), F32)
    one_a = ar_first(one_p, one_in, AR_ONE)
    one_b = ar_second(one_p, one_in, one_all, AR_ONE, one_a)

    classes = grad.shape[0]
    total = None
    for i in range(2):
        x2_y[i].wait_recv()
        rs = ds(y * half + i * quarter, quarter)
        act = (x2p[:, rs] + x2_in[:, pl.ds(i * quarter, quarter)]).astype(BF16)
        part = dot(gbt[:, rs], act, NT)
        total = part if total is None else total + part
    two_p[pl.ds(0, classes)] = total
    two_p[pl.ds(classes, two_p.shape[0] - classes)] = jnp.zeros((two_p.shape[0] - classes, two_p.shape[1]), F32)
    two_a = ar_first(two_p, two_in, AR_TWO)
    one_c = ar_third(one_all, one_tot, AR_ONE, one_b)
    two_b = ar_second(two_p, two_in, two_all, AR_TWO, two_a)
    two_c = ar_third(two_all, two_tot, AR_TWO, two_b)
    one_c.wait_recv()
    dw1_out[...] = one_tot[pl.ds(0, feat_in)]
    two_c.wait_recv()
    dw2t_out[...] = two_tot[pl.ds(0, classes)]

    @pl.when(diag)
    def _():
        h_near.wait_send()
        x1_near.wait_send()

    @pl.when(jnp.logical_not(diag))
    def _():
        h_far.wait_send()
        x1_far.wait_send()
        x1_far2.wait_send()

    for copy in [*ht_d2d, *x1_y, *x1_d2d, *dz_d2d, dz_x_copy, *x2_y, one_a, *one_b, one_c, two_a, *two_b, two_c]:
        copy.wait_send()


def solution(mesh):
    def local_step(adj, feat, w_one, w_two, grad):
        rows, cols = adj.shape
        feat_in, hidden = w_one.shape
        classes = w_two.shape[1]
        half = rows // 2
        fpad, cpad = -(-feat_in // 16) * 16, -(-classes // 16) * 16
        vmem = pltpu.VMEM
        dw1, dw2t = pl.pallas_call(
            gcn_kernel,
            out_shape=(jax.ShapeDtypeStruct((feat_in, hidden), F32), jax.ShapeDtypeStruct((classes, hidden), F32)),
            in_specs=[pl.BlockSpec(memory_space=pltpu.HBM)] * 5,
            out_specs=(pl.BlockSpec(memory_space=vmem), pl.BlockSpec(memory_space=vmem)),
            scratch_shapes=[
                vmem((rows, cols), BF16),
                vmem((feat_in, cols), BF16),
                vmem((classes, rows), F32),
                vmem((feat_in, hidden), BF16),
                vmem((classes, hidden), BF16),
                vmem((classes, rows), BF16),
                vmem((hidden, rows), BF16),
                vmem((hidden, cols), F32),
                vmem((hidden, rows), F32),
                vmem((hidden, half), F32),
                vmem((hidden, half), F32),
                vmem((feat_in, rows), F32),
                vmem((feat_in, half), F32),
                vmem((feat_in, half), BF16),
                vmem((feat_in, cols), BF16),
                vmem((hidden, cols), BF16),
                vmem((hidden, rows), F32),
                vmem((hidden, half), F32),
                vmem((fpad, hidden), F32),
                vmem((fpad // 2, hidden), F32),
                vmem((4, fpad // 2, hidden), F32),
                vmem((fpad, hidden), F32),
                vmem((cpad, hidden), F32),
                vmem((cpad // 2, hidden), F32),
                vmem((4, cpad // 2, hidden), F32),
                vmem((cpad, hidden), F32),
                pltpu.SemaphoreType.DMA((A_CHUNKS,)),
                pltpu.SemaphoreType.DMA((4,)),
                pltpu.SemaphoreType.DMA((N_REMOTE,)),
                pltpu.SemaphoreType.DMA((N_REMOTE,)),
            ],
            compiler_params=pltpu.CompilerParams(
                collective_id=0, has_side_effects=True, vmem_limit_bytes=60 * 1024 * 1024),
        )(adj, feat.T, w_one, w_two.T, grad.T)
        return dw1, dw2t.T

    return jax.shard_map(
        local_step, mesh=mesh,
        in_specs=(P("rows", "rep"), P("rows", None), P(), P(), P("rows", None)),
        out_specs=(P(), P()), check_vma=False)
```

time: 265 us -> 77 us (0.29)
  blocking collectives: 132 us -> 0 us
  Pallas kernels: 0 us -> 73.2 us
  waiting for transfers between devices: 65.6 us -> 0 us
  matrix products: 38.3 us -> 0 us
  between operations: 13.9 us -> 0.64 us
  starting transfers between devices: 11.1 us -> 0 us
    psum x3 -> x0, blocking collectives: 111 us -> none  [the longest x1 57.7 us: local_step(): lax.psum(jnp.dot(adj_blk, hidden_range, preferred_element_type=jnp.float3...]
    pallas_call x0 -> x1, Pallas kernels: none -> 73.2 us  [local_step(): pl.pallas_call(gcn_kernel, out_shape=(jax.ShapeDtypeStruct((feat_in, hidd...]
    dot_general x6 -> x0, matrix products: 38.3 us -> none  [the longest x1 12.3 us: local_step(): jnp.dot(adj_blk, hidden_range, preferred_element_type=jnp.float32)]
    reduce_scatter x1 -> x0, waiting for transfers between devices: 28.5 us -> none  [local_step(): lax.psum_scatter(d_partial, 'rows', scatter_dimension=0, tiled=True)]
    all_gather x1 -> x0, blocking collectives: 20.9 us -> none  [column_rows(): return lax.all_gather(arrived, 'rows', axis=0, tiled=True)]
    psum x1 -> x0, waiting for transfers between devices: 19 us -> none  [local_step(): return (lax.psum(dw_one, both_axes), lax.psum(dw_two, both_axes))]
    all_gather x1 -> x0, waiting for transfers between devices: 18 us -> none  [column_rows(): return lax.all_gather(arrived, 'rows', axis=0, tiled=True)]
    ppermute x3 -> x0, starting transfers between devices: 10.8 us -> none  [the longest x1 9.47 us: local_step(): d_hidden = lax.ppermute(d_piece, both_axes, perm=to_blocks)]
  transfers between devices with their start and end apart: 6 -> 0, of which waited for: 3 -> 0; matrix products, arithmetic and copies ran while one was open for 9% -> 0% of each run, Pallas kernels for 0% -> 0%
where the time goes in v1:
time: 77 us; the launch traced here: 76.8 us
  Pallas kernels  73.2 us (95%)
  local copies, waits for them, and re-layouts  2.97 us (4%)
    pallas_call x1, Pallas kernels, local_step(): pl.pallas_call(gcn_kernel, out_shape=(jax.ShapeDtypeStruct((feat_in, hidd...  73.2 us
    unnamed x2, local copies, waits for them, and re-layouts  2.97 us

profile of v1, /device:TPU:0, one launch (start us, length us, event | category | flops | bytes accessed | tf_op | source)
XLA Modules:
  0.0 76.8 jit_solution(4761200762172674031)
XLA Ops:
  0.6 73.2 %shard_map.68 = (f32[100,256]{1,0:T(8,128)}, f32[47,256]{1,0:T(8,128)}) custom-call(bf16[2048,4096]{1,0:T(8,128)(2,1)} %adj.1, bf16[100,2048]{1,0:T(8,128)(2,1)} %bitcast.4, bf16[100,256]{1,0:T(8,128)(2,1)} %w_one.1, bf16[47,256]{1,0:T(8,128)(2,1)} %bitcast.7, f32[47,2048]{1,0:T(8,128)} %bitcast.5), custom_call_target="tpu_custom_call" | custom-call | tf_op jit(solution)/shard_map/pallas_call | solution.py:273
  73.9 1.5 %copy.9 = f32[100,256]{1,0:T(8,128)} copy(f32[100,256]{1,0:T(8,128)} %get-tuple-element.8) | data formatting | bytes 204800
  75.4 1.4 %copy.10 = f32[256,47]{0,1:T(8,128)} copy(f32[256,47]{0,1:T(8,128)} %bitcast.6) | data formatting | bytes 96256

commit v2 on v0

v2 whole, which is shorter than its diff:
```python
import itertools

import jax
import jax.numpy as jnp
from jax import lax
from jax.experimental import pallas as pl
from jax.experimental.pallas import tpu as pltpu
from jax.sharding import PartitionSpec as P

MESH = pl.DeviceIdType.MESH
F32 = jnp.float32
BF16 = jnp.bfloat16
NN = (((1,), (0,)), ((), ()))
NT = (((1,), (1,)), ((), ()))
TN = (((0,), (0,)), ((), ()))
SUBS = 4
N_SEND = 64
H_R, HT_R, X1Y_R, X1G_R, X1D_R, DZD_R, DZX_R, X2Y_R, ONE_R, TWO_R, N_RECV = 0, 4, 8, 12, 20, 28, 30, 34, 38, 42, 47


def dot(lhs, rhs, dims):
    return lax.dot_general(lhs, rhs, dims, preferred_element_type=F32)


def ds(start, size, align=128):
    return pl.ds(pl.multiple_of(start, align), size)


def gcn_kernel(
    adj, feat, w_one, w_two, grad, dw1_out, dw2t_out,
    a_v, ht, hs, g_v, w1_v, w2_v, gbt, dyt, dzp, dz_in, dz_s, dz_x,
    x1p, x1_in, x1s, x1t, z1t, x2p, x2_in,
    one_p, one_in, one_s, one_x, one_sx, one_y, one_tot, two_p, two_in, two_all, two_tot,
    a_sem, l_sem, send_sem, recv_sem,
):
    y = lax.axis_index("rep")
    r = lax.axis_index("rows")
    x, c = r // 2, lax.rem(r, 2)
    diag = x == y
    off = jnp.logical_not(diag)
    peer = (y, 2 * x + 1 - c)
    xn = (y, 2 * (1 - x) + c)
    yn = (1 - y, r)
    opp = (1 - y, 2 * (1 - x) + c)
    user = (x, 2 * (1 - x) + c)
    rows, cols = a_v.shape
    half, quarter = rows // 2, rows // 4
    sub = half // SUBS
    feat_in, classes = feat.shape[0], grad.shape[0]
    my_cols, peer_cols = c * rows, (1 - c) * rows
    send_ids = itertools.count()
    sent, sent_diag, sent_off = [], [], []

    def rcopy(src, dst, recv, dev, group=sent):
        copy = pltpu.make_async_remote_copy(
            src_ref=src, dst_ref=dst, send_sem=send_sem.at[next(send_ids)], recv_sem=recv_sem.at[recv],
            device_id=dev, device_id_type=MESH)
        group.append(copy)
        return copy

    def wait_recv(dst, recv):
        pltpu.make_async_remote_copy(
            src_ref=dst, dst_ref=dst, send_sem=send_sem.at[0], recv_sem=recv_sem.at[recv],
            device_id=peer, device_id_type=MESH).wait_recv()

    hs_load = pltpu.make_async_copy(feat.at[:, ds(jnp.where(diag, 0, half), half)], hs, l_sem.at[4])
    h_load = pltpu.make_async_copy(feat, ht.at[:, ds(my_cols, rows)], l_sem.at[3])
    hs_load.start()

    @pl.when(diag)
    def _():
        h_load.start()

    g_load = pltpu.make_async_copy(grad, g_v, l_sem.at[0])
    w1_load = pltpu.make_async_copy(w_one, w1_v, l_sem.at[1])
    w2_load = pltpu.make_async_copy(w_two, w2_v, l_sem.at[2])
    g_load.start()
    w1_load.start()
    w2_load.start()
    own0, other0 = y * half, (1 - y) * half
    a_rows = [ds(other0, quarter), ds(other0 + quarter, quarter), ds(own0, quarter), ds(own0 + quarter, quarter)]
    a_loads = [pltpu.make_async_copy(adj.at[rs], a_v.at[rs], a_sem.at[i]) for i, rs in enumerate(a_rows)]
    for load in a_loads:
        load.start()

    barrier = pltpu.get_barrier_semaphore()
    for dev in (peer, xn, yn, opp):
        pl.semaphore_signal(barrier, inc=1, device_id=dev, device_id_type=MESH)
    pl.semaphore_wait(barrier, 4)

    hs_load.wait()
    side = jnp.where(diag, 0, 1)
    for i in range(2):
        rcopy(hs.at[:, pl.ds(i * quarter, quarter)],
              ht.at[:, ds(my_cols + side * half + i * quarter, quarter)], H_R + 2 * side + i, user).start()

    def h_piece(k):
        return ht.at[:, ds(my_cols + k * quarter, quarter)]

    h_fwd = [rcopy(h_piece(k), h_piece(k), HT_R + k, peer) for k in range(4)]

    @pl.when(diag)
    def _():
        h_load.wait()
        for k in range(4):
            h_fwd[k].start()

    g_load.wait()
    w2_load.wait()
    gbt[...] = g_v[...].astype(BF16)
    dyt[...] = dot(w2_v[...], gbt[...], TN).astype(BF16)

    @pl.when(off)
    def _():
        for k in (0, 2, 1, 3):
            wait_recv(h_piece(k), H_R + k)
            h_fwd[k].start()

    own_block, peer_block = ds(my_cols, rows), ds(peer_cols, rows)
    for i in range(2):
        a_loads[i].wait()
        x1p[:, a_rows[i]] = dot(ht[:, own_block], a_v[a_rows[i], own_block], NT)
    for k in range(4):
        h_fwd[k].wait_recv()
    x1_y = []
    for i in range(2):
        x1p[:, a_rows[i]] += dot(ht[:, peer_block], a_v[a_rows[i], peer_block], NT)
        for j in range(2 * i, 2 * i + 2):
            x1_y.append(rcopy(x1p.at[:, ds(other0 + j * sub, sub)], x1_in.at[:, pl.ds(j * sub, sub)], X1Y_R + j, yn))
            x1_y[-1].start()
    for i in range(2, 4):
        a_loads[i].wait()
        x1p[:, a_rows[i]] = dot(ht[...], a_v[a_rows[i], :], NT)

    dz_d2d = []

    def backward(start):
        cs = ds(start, half)
        dzp[:, cs] = dot(dyt[...], a_v[:, cs], NN)

    def mine(ref, h, i):
        return ref.at[:, ds(my_cols + h * half + i * sub, sub)]

    x1_fwd = {(h, i): rcopy(mine(x1t, hv, i), mine(x1t, hv, i), X1D_R + 4 * h + i, peer)
              for h, hv in ((0, x), (1, 1 - x)) for i in range(SUBS)}
    x1_user, x1_col = [], []

    def sum_x1(i):
        x1_y[i].wait_recv()
        cs = pl.ds(i * sub, sub)
        act = (x1p[:, ds(own0 + i * sub, sub)] + x1_in[:, cs]).astype(BF16)
        x1s[:, cs] = act
        x1_user.append(rcopy(x1s.at[:, cs], mine(x1t, y, i), X1G_R + 4 * y + i, user))
        x1_col.append(rcopy(x1s.at[:, cs], mine(x1t, y, i), X1G_R + 4 * y + i, yn, sent_off))
        x1_user[-1].start()

        @pl.when(diag)
        def _():
            mine(x1t, y, i)[...] = act
            x1_fwd[0, i].start()

        @pl.when(off)
        def _():
            x1_col[i].start()

    for i in range(2):
        backward(peer_cols + i * half)
        dz_d2d.append(rcopy(dzp.at[:, ds(peer_cols + i * half, half)], dz_in.at[:, pl.ds(i * half, half)], DZD_R + i, peer))
        dz_d2d[-1].start()
    sum_x1(0)
    backward(my_cols)
    sum_x1(1)
    backward(my_cols + half)
    sum_x1(2)
    for copy in dz_d2d:
        copy.wait_recv()
    dz_s[...] = dzp[:, ds(my_cols + (1 - x) * half, half)] + dz_in[:, ds((1 - x) * half, half)]
    sum_x1(3)
    dz_x_copies = []
    for i in range(SUBS):
        cs = pl.ds(i * sub, sub)
        dz_x_copies.append(rcopy(dz_s.at[:, cs], dz_x.at[:, cs], DZX_R + i, xn))
        dz_x_copies[-1].start()

    w1_load.wait()

    def hidden(start, size):
        cs = ds(start, size)
        z1t[:, cs] = jnp.maximum(dot(w1_v[...], x1t[:, cs], TN), 0.0).astype(BF16)

    for i in range(SUBS):
        @pl.when(off)
        def _():
            wait_recv(mine(x1t, x, i), X1G_R + 4 * x + i)
            x1_fwd[0, i].start()
    hidden(my_cols + x * half, half)
    for i in range(SUBS):
        x1_fwd[0, i].wait_recv()
    hidden(peer_cols + x * half, half)
    first_own, first_peer = ds(my_cols + x * half, half), ds(peer_cols + x * half, half)
    for i in range(SUBS):
        rs = a_rows[i]
        x2p[:, rs] = dot(z1t[:, first_own], a_v[rs, first_own], NT) + dot(z1t[:, first_peer], a_v[rs, first_peer], NT)
        wait_recv(mine(x1t, 1 - x, i), X1G_R + 4 * (1 - x) + i)
        x1_fwd[1, i].start()
        hidden(my_cols + (1 - x) * half + i * sub, sub)
    for i in range(SUBS):
        x1_fwd[1, i].wait_recv()
        hidden(peer_cols + (1 - x) * half + i * sub, sub)
    last_own, last_peer = ds(my_cols + (1 - x) * half, half), ds(peer_cols + (1 - x) * half, half)
    x2_y = []
    for i in range(SUBS):
        rs = a_rows[i]
        x2p[:, rs] += dot(z1t[:, last_own], a_v[rs, last_own], NT) + dot(z1t[:, last_peer], a_v[rs, last_peer], NT)
        if i < 2:
            for j in range(2 * i, 2 * i + 2):
                x2_y.append(rcopy(x2p.at[:, ds(other0 + j * sub, sub)], x2_in.at[:, pl.ds(j * sub, sub)], X2Y_R + j, yn))
                x2_y[-1].start()

    dw1 = None
    for i in range(SUBS):
        dz_x_copies[i].wait_recv()
        cs = ds(my_cols + x * half + i * sub, sub)
        d_hidden = (dzp[:, cs] + dz_in[:, ds(x * half + i * sub, sub)]) + dz_x[:, pl.ds(i * sub, sub)]
        d_pre = jnp.where(z1t[:, cs].astype(F32) > 0.0, d_hidden, 0.0).astype(BF16)
        part = dot(x1t[:, cs], d_pre, NT)
        dw1 = part if dw1 is None else dw1 + part
    one_p[pl.ds(0, feat_in)] = dw1
    one_p[pl.ds(feat_in, one_p.shape[0] - feat_in)] = jnp.zeros((one_p.shape[0] - feat_in, one_p.shape[1]), F32)

    n_one = one_p.shape[0] // 2
    one_a = rcopy(one_p.at[ds((1 - c) * n_one, n_one, 8)], one_in, ONE_R, peer)
    one_a.start()
    one_a.wait_recv()
    one_s[...] = one_p[ds(c * n_one, n_one, 8)] + one_in[...]
    one_b = rcopy(one_s, one_x, ONE_R + 1, xn)
    one_b.start()
    one_b.wait_recv()
    one_sx[...] = one_s[...] + one_x[...]
    one_c = rcopy(one_sx, one_y, ONE_R + 2, yn)
    one_c.start()

    dw2 = None
    for i in range(SUBS):
        x2_y[i].wait_recv()
        rs = ds(own0 + i * sub, sub)
        act = (x2p[:, rs] + x2_in[:, pl.ds(i * sub, sub)]).astype(BF16)
        part = dot(gbt[:, rs], act, NT)
        dw2 = part if dw2 is None else dw2 + part
    two_p[pl.ds(0, classes)] = dw2
    two_p[pl.ds(classes, two_p.shape[0] - classes)] = jnp.zeros((two_p.shape[0] - classes, two_p.shape[1]), F32)

    n_two = two_p.shape[0] // 2
    chip = 2 * x + y
    two_a = rcopy(two_p.at[ds((1 - c) * n_two, n_two, 8)], two_in, TWO_R, peer)
    two_a.start()
    one_c.wait_recv()
    one_mine = ds(c * n_one, n_one, 8)
    one_tot[one_mine] = one_sx[...] + one_y[...]
    one_d = rcopy(one_tot.at[one_mine], one_tot.at[one_mine], ONE_R + 3, peer)
    one_d.start()
    two_a.wait_recv()
    two_all[chip] = two_p[ds(c * n_two, n_two, 8)] + two_in[...]
    two_b = [rcopy(two_all.at[chip], two_all.at[chip], TWO_R + 1 + i, dev) for i, dev in enumerate((opp, xn, yn))]
    for copy in two_b:
        copy.start()
    one_d.wait_recv()
    dw1_out[...] = one_tot[pl.ds(0, feat_in)]
    for copy in two_b:
        copy.wait_recv()
    two_mine = ds(c * n_two, n_two, 8)
    two_tot[two_mine] = (two_all[0] + two_all[1]) + (two_all[2] + two_all[3])
    two_c = rcopy(two_tot.at[two_mine], two_tot.at[two_mine], TWO_R + 4, peer)
    two_c.start()
    two_c.wait_recv()
    dw2t_out[...] = two_tot[pl.ds(0, classes)]

    for copy in sent:
        copy.wait_send()

    @pl.when(off)
    def _():
        for copy in sent_off:
            copy.wait_send()


def solution(mesh):
    def local_step(adj, feat, w_one, w_two, grad):
        rows, cols = adj.shape
        feat_in, hidden = w_one.shape
        classes = w_two.shape[1]
        half = rows // 2
        fpad, cpad = -(-feat_in // 16) * 16, -(-classes // 16) * 16
        vmem = pltpu.VMEM
        one_half = vmem((fpad // 2, hidden), F32)
        dw1, dw2t = pl.pallas_call(
            gcn_kernel,
            out_shape=(jax.ShapeDtypeStruct((feat_in, hidden), F32), jax.ShapeDtypeStruct((classes, hidden), F32)),
            in_specs=[pl.BlockSpec(memory_space=pltpu.HBM)] * 5,
            out_specs=(pl.BlockSpec(memory_space=vmem), pl.BlockSpec(memory_space=vmem)),
            scratch_shapes=[
                vmem((rows, cols), BF16),
                vmem((feat_in, cols), BF16),
                vmem((feat_in, half), BF16),
                vmem((classes, rows), F32),
                vmem((feat_in, hidden), BF16),
                vmem((classes, hidden), BF16),
                vmem((classes, rows), BF16),
                vmem((hidden, rows), BF16),
                vmem((hidden, cols), F32),
                vmem((hidden, rows), F32),
                vmem((hidden, half), F32),
                vmem((hidden, half), F32),
                vmem((feat_in, rows), F32),
                vmem((feat_in, half), F32),
                vmem((feat_in, half), BF16),
                vmem((feat_in, cols), BF16),
                vmem((hidden, cols), BF16),
                vmem((hidden, rows), F32),
                vmem((hidden, half), F32),
                vmem((fpad, hidden), F32),
                *[one_half] * 5,
                vmem((fpad, hidden), F32),
                vmem((cpad, hidden), F32),
                vmem((cpad // 2, hidden), F32),
                vmem((4, cpad // 2, hidden), F32),
                vmem((cpad, hidden), F32),
                pltpu.SemaphoreType.DMA((4,)),
                pltpu.SemaphoreType.DMA((5,)),
                pltpu.SemaphoreType.DMA((N_SEND,)),
                pltpu.SemaphoreType.DMA((N_RECV,)),
            ],
            compiler_params=pltpu.CompilerParams(
                collective_id=0, has_side_effects=True, vmem_limit_bytes=60 * 1024 * 1024),
        )(adj, feat.T, w_one, w_two.T, grad.T)
        return dw1, dw2t.T

    return jax.shard_map(
        local_step, mesh=mesh,
        in_specs=(P("rows", "rep"), P("rows", None), P(), P(), P("rows", None)),
        out_specs=(P(), P()), check_vma=False)
```

time: 265 us -> 69.1 us (0.26)
  blocking collectives: 132 us -> 0 us
  waiting for transfers between devices: 65.6 us -> 0 us
  Pallas kernels: 0 us -> 65.3 us
  matrix products: 38.3 us -> 0 us
  between operations: 13.9 us -> 0.64 us
  starting transfers between devices: 11.1 us -> 0 us
    psum x3 -> x0, blocking collectives: 111 us -> none  [the longest x1 57.7 us: local_step(): lax.psum(jnp.dot(adj_blk, hidden_range, preferred_element_type=jnp.float3...]
    pallas_call x0 -> x1, Pallas kernels: none -> 65.3 us  [local_step(): pl.pallas_call(gcn_kernel, out_shape=(jax.ShapeDtypeStruct((feat_in, hidd...]
    dot_general x6 -> x0, matrix products: 38.3 us -> none  [the longest x1 12.3 us: local_step(): jnp.dot(adj_blk, hidden_range, preferred_element_type=jnp.float32)]
    reduce_scatter x1 -> x0, waiting for transfers between devices: 28.5 us -> none  [local_step(): lax.psum_scatter(d_partial, 'rows', scatter_dimension=0, tiled=True)]
    all_gather x1 -> x0, blocking collectives: 20.9 us -> none  [column_rows(): return lax.all_gather(arrived, 'rows', axis=0, tiled=True)]
    psum x1 -> x0, waiting for transfers between devices: 19 us -> none  [local_step(): return (lax.psum(dw_one, both_axes), lax.psum(dw_two, both_axes))]
    all_gather x1 -> x0, waiting for transfers between devices: 18 us -> none  [column_rows(): return lax.all_gather(arrived, 'rows', axis=0, tiled=True)]
    ppermute x3 -> x0, starting transfers between devices: 10.8 us -> none  [the longest x1 9.47 us: local_step(): d_hidden = lax.ppermute(d_piece, both_axes, perm=to_blocks)]
  transfers between devices with their start and end apart: 6 -> 0, of which waited for: 3 -> 0; matrix products, arithmetic and copies ran while one was open for 9% -> 0% of each run, Pallas kernels for 0% -> 0%
where the time goes in v2:
time: 69.1 us; the launch traced here: 68.9 us
  Pallas kernels  65.3 us (95%)
  local copies, waits for them, and re-layouts  2.97 us (4%)
    pallas_call x1, Pallas kernels, local_step(): pl.pallas_call(gcn_kernel, out_shape=(jax.ShapeDtypeStruct((feat_in, hidd...  65.3 us
    unnamed x2, local copies, waits for them, and re-layouts  2.97 us

profile of v2, /device:TPU:0, one launch (start us, length us, event | category | flops | bytes accessed | tf_op | source)
XLA Modules:
  0.0 68.9 jit_solution(9440544488982135455)
XLA Ops:
  0.6 65.3 %shard_map.68 = (f32[100,256]{1,0:T(8,128)}, f32[47,256]{1,0:T(8,128)}) custom-call(bf16[2048,4096]{1,0:T(8,128)(2,1)} %adj.1, bf16[100,2048]{1,0:T(8,128)(2,1)} %bitcast.4, bf16[100,256]{1,0:T(8,128)(2,1)} %w_one.1, bf16[47,256]{1,0:T(8,128)(2,1)} %bitcast.7, f32[47,2048]{1,0:T(8,128)} %bitcast.5), custom_call_target="tpu_custom_call" | custom-call | tf_op jit(solution)/shard_map/pallas_call | solution.py:296
  66.0 1.5 %copy.9 = f32[100,256]{1,0:T(8,128)} copy(f32[100,256]{1,0:T(8,128)} %get-tuple-element.8) | data formatting | bytes 204800
  67.5 1.4 %copy.10 = f32[256,47]{0,1:T(8,128)} copy(f32[256,47]{0,1:T(8,128)} %bitcast.6) | data formatting | bytes 96256

commit v3 on v2

--- a/solution.py
+++ b/solution.py
@@ -63,9 +63,12 @@
             src_ref=dst, dst_ref=dst, send_sem=send_sem.at[0], recv_sem=recv_sem.at[recv],
             device_id=peer, device_id_type=MESH).wait_recv()
 
-    hs_load = pltpu.make_async_copy(feat.at[:, ds(jnp.where(diag, 0, half), half)], hs, l_sem.at[4])
+    side = jnp.where(diag, 0, 1)
+    hs_loads = [pltpu.make_async_copy(feat.at[:, ds((2 * w + side) * quarter, quarter)],
+                                      hs.at[:, pl.ds(w * quarter, quarter)], l_sem.at[4 + w]) for w in range(2)]
     h_load = pltpu.make_async_copy(feat, ht.at[:, ds(my_cols, rows)], l_sem.at[3])
-    hs_load.start()
+    for load in hs_loads:
+        load.start()
 
     @pl.when(diag)
     def _():
@@ -74,29 +77,36 @@
     g_load = pltpu.make_async_copy(grad, g_v, l_sem.at[0])
     w1_load = pltpu.make_async_copy(w_one, w1_v, l_sem.at[1])
     w2_load = pltpu.make_async_copy(w_two, w2_v, l_sem.at[2])
-    g_load.start()
-    w1_load.start()
-    w2_load.start()
     own0, other0 = y * half, (1 - y) * half
     a_rows = [ds(other0, quarter), ds(other0 + quarter, quarter), ds(own0, quarter), ds(own0 + quarter, quarter)]
-    a_loads = [pltpu.make_async_copy(adj.at[rs], a_v.at[rs], a_sem.at[i]) for i, rs in enumerate(a_rows)]
-    for load in a_loads:
+    a_loads = []
+    for i, start in enumerate((other0, other0 + quarter, own0, own0 + quarter)):
+        for j in range(2):
+            rs = ds(start + j * sub, sub)
+            a_loads.append(pltpu.make_async_copy(adj.at[rs], a_v.at[rs], a_sem.at[2 * i + j]))
+    for load in a_loads[:4]:
         load.start()
+
+    def wait_a(i):
+        a_loads[2 * i].wait()
+        a_loads[2 * i + 1].wait()
 
     barrier = pltpu.get_barrier_semaphore()
     for dev in (peer, xn, yn, opp):
         pl.semaphore_signal(barrier, inc=1, device_id=dev, device_id_type=MESH)
     pl.semaphore_wait(barrier, 4)
 
-    hs_load.wait()
-    side = jnp.where(diag, 0, 1)
-    for i in range(2):
-        rcopy(hs.at[:, pl.ds(i * quarter, quarter)],
-              ht.at[:, ds(my_cols + side * half + i * quarter, quarter)], H_R + 2 * side + i, user).start()
-
     def h_piece(k):
         return ht.at[:, ds(my_cols + k * quarter, quarter)]
 
+    for w in range(2):
+        hs_loads[w].wait()
+        rcopy(hs.at[:, pl.ds(w * quarter, quarter)], h_piece(2 * w + side), H_R + 2 * w + side, user).start()
+
+    for load in a_loads[4:]:
+        load.start()
+    for load in (g_load, w1_load, w2_load):
+        load.start()
     h_fwd = [rcopy(h_piece(k), h_piece(k), HT_R + k, peer) for k in range(4)]
 
     @pl.when(diag)
@@ -105,31 +115,50 @@
         for k in range(4):
             h_fwd[k].start()
 
-    g_load.wait()
-    w2_load.wait()
-    gbt[...] = g_v[...].astype(BF16)
-    dyt[...] = dot(w2_v[...], gbt[...], TN).astype(BF16)
-
-    @pl.when(off)
-    def _():
-        for k in (0, 2, 1, 3):
-            wait_recv(h_piece(k), H_R + k)
-            h_fwd[k].start()
-
-    own_block, peer_block = ds(my_cols, rows), ds(peer_cols, rows)
+    x1_y = []
+
+    def add_x1(i, cs, first=False):
+        part = dot(ht[:, cs], a_v[a_rows[i], cs], NT)
+        x1p[:, a_rows[i]] = part if first else x1p[:, a_rows[i]] + part
+
+    for j in range(SUBS):
+        x1_y.append(rcopy(x1p.at[:, ds(other0 + j * sub, sub)], x1_in.at[:, pl.ds(j * sub, sub)], X1Y_R + j, yn))
+
+    def send_x1(i, role):
+        @pl.when(role)
+        def _():
+            x1_y[2 * i].start()
+            x1_y[2 * i + 1].start()
+
+    def forward_h(w):
+        @pl.when(off)
+        def _():
+            for k in (2 * w, 2 * w + 1):
+                wait_recv(h_piece(k), H_R + k)
+                h_fwd[k].start()
+
+    waves = [(ds(my_cols + w * half, half), ds(peer_cols + w * half, half)) for w in range(2)]
+    forward_h(0)
     for i in range(2):
-        a_loads[i].wait()
-        x1p[:, a_rows[i]] = dot(ht[:, own_block], a_v[a_rows[i], own_block], NT)
-    for k in range(4):
+        wait_a(i)
+        add_x1(i, waves[0][0], True)
+    for k in range(2):
         h_fwd[k].wait_recv()
-    x1_y = []
     for i in range(2):
-        x1p[:, a_rows[i]] += dot(ht[:, peer_block], a_v[a_rows[i], peer_block], NT)
-        for j in range(2 * i, 2 * i + 2):
-            x1_y.append(rcopy(x1p.at[:, ds(other0 + j * sub, sub)], x1_in.at[:, pl.ds(j * sub, sub)], X1Y_R + j, yn))
-            x1_y[-1].start()
+        add_x1(i, waves[0][1])
+    forward_h(1)
+    add_x1(0, waves[1][0])
+    for k in range(2, 4):
+        h_fwd[k].wait_recv()
+    add_x1(0, waves[1][1])
+    send_x1(0, off)
+    add_x1(1, waves[1][0])
+    add_x1(1, waves[1][1])
+    send_x1(0, diag)
+    send_x1(1, diag)
+    send_x1(1, off)
     for i in range(2, 4):
-        a_loads[i].wait()
+        wait_a(i)
         x1p[:, a_rows[i]] = dot(ht[...], a_v[a_rows[i], :], NT)
 
     dz_d2d = []
@@ -142,17 +171,20 @@
         return ref.at[:, ds(my_cols + h * half + i * sub, sub)]
 
     x1_fwd = {(h, i): rcopy(mine(x1t, hv, i), mine(x1t, hv, i), X1D_R + 4 * h + i, peer)
-              for h, hv in ((0, x), (1, 1 - x)) for i in range(SUBS)}
+              for h, hv in ((0, y), (1, 1 - y)) for i in range(SUBS)}
     x1_user, x1_col = [], []
+
+    for i in range(SUBS):
+        piece = x1s.at[:, pl.ds(i * sub, sub)]
+        x1_user.append(rcopy(piece, mine(x1t, y, i), X1G_R + 4 * y + i, user))
+        x1_col.append(rcopy(piece, mine(x1t, y, i), X1G_R + 4 * y + i, yn, sent_off))
 
     def sum_x1(i):
         x1_y[i].wait_recv()
         cs = pl.ds(i * sub, sub)
         act = (x1p[:, ds(own0 + i * sub, sub)] + x1_in[:, cs]).astype(BF16)
         x1s[:, cs] = act
-        x1_user.append(rcopy(x1s.at[:, cs], mine(x1t, y, i), X1G_R + 4 * y + i, user))
-        x1_col.append(rcopy(x1s.at[:, cs], mine(x1t, y, i), X1G_R + 4 * y + i, yn, sent_off))
-        x1_user[-1].start()
+        x1_user[i].start()
 
         @pl.when(diag)
         def _():
@@ -162,16 +194,20 @@
         @pl.when(off)
         def _():
             x1_col[i].start()
+
+    g_load.wait()
+    w2_load.wait()
+    gbt[...] = g_v[...].astype(BF16)
+    dyt[...] = dot(w2_v[...], gbt[...], TN).astype(BF16)
 
     for i in range(2):
         backward(peer_cols + i * half)
         dz_d2d.append(rcopy(dzp.at[:, ds(peer_cols + i * half, half)], dz_in.at[:, pl.ds(i * half, half)], DZD_R + i, peer))
         dz_d2d[-1].start()
-    sum_x1(0)
+        sum_x1(i)
     backward(my_cols)
-    sum_x1(1)
+    sum_x1(2)
     backward(my_cols + half)
-    sum_x1(2)
     for copy in dz_d2d:
         copy.wait_recv()
     dz_s[...] = dzp[:, ds(my_cols + (1 - x) * half, half)] + dz_in[:, ds((1 - x) * half, half)]
@@ -180,42 +216,70 @@
     for i in range(SUBS):
         cs = pl.ds(i * sub, sub)
         dz_x_copies.append(rcopy(dz_s.at[:, cs], dz_x.at[:, cs], DZX_R + i, xn))
-        dz_x_copies[-1].start()
-
+
+    def send_dz(role):
+        @pl.when(role)
+        def _():
+            for copy in dz_x_copies:
+                copy.start()
+
+    send_dz(off)
     w1_load.wait()
 
     def hidden(start, size):
         cs = ds(start, size)
         z1t[:, cs] = jnp.maximum(dot(w1_v[...], x1t[:, cs], TN), 0.0).astype(BF16)
 
-    for i in range(SUBS):
+    halves = (y * half, (1 - y) * half)
+
+    def own_piece(i):
         @pl.when(off)
         def _():
-            wait_recv(mine(x1t, x, i), X1G_R + 4 * x + i)
+            wait_recv(mine(x1t, y, i), X1G_R + 4 * y + i)
             x1_fwd[0, i].start()
-    hidden(my_cols + x * half, half)
-    for i in range(SUBS):
+
+        wait_recv(mine(x1t, 1 - y, i), X1G_R + 4 * (1 - y) + i)
+        x1_fwd[1, i].start()
+        for h in halves:
+            hidden(my_cols + h + i * sub, sub)
+
+    def peer_piece(i):
         x1_fwd[0, i].wait_recv()
-    hidden(peer_cols + x * half, half)
-    first_own, first_peer = ds(my_cols + x * half, half), ds(peer_cols + x * half, half)
-    for i in range(SUBS):
-        rs = a_rows[i]
-        x2p[:, rs] = dot(z1t[:, first_own], a_v[rs, first_own], NT) + dot(z1t[:, first_peer], a_v[rs, first_peer], NT)
-        wait_recv(mine(x1t, 1 - x, i), X1G_R + 4 * (1 - x) + i)
-        x1_fwd[1, i].start()
-        hidden(my_cols + (1 - x) * half + i * sub, sub)
-    for i in range(SUBS):
         x1_fwd[1, i].wait_recv()
-        hidden(peer_cols + (1 - x) * half + i * sub, sub)
-    last_own, last_peer = ds(my_cols + (1 - x) * half, half), ds(peer_cols + (1 - x) * half, half)
+        for h in halves:
+            hidden(peer_cols + h + i * sub, sub)
+
+    def part_x2(rs, block, group):
+        total = None
+        for h in halves:
+            cs = ds(block + h + group * quarter, quarter)
+            part = dot(z1t[:, cs], a_v[rs, cs], NT)
+            total = part if total is None else total + part
+        return total
+
+    own_piece(0)
+    send_dz(diag)
+    own_piece(1)
+    peer_piece(0)
+    peer_piece(1)
+    x2p[:, a_rows[0]] = part_x2(a_rows[0], my_cols, 0) + part_x2(a_rows[0], peer_cols, 0)
+    own_piece(2)
+    x2p[:, a_rows[1]] = part_x2(a_rows[1], my_cols, 0) + part_x2(a_rows[1], peer_cols, 0)
+    own_piece(3)
+    peer_piece(2)
+    x2p[:, a_rows[0]] += part_x2(a_rows[0], my_cols, 1)
+    peer_piece(3)
     x2_y = []
-    for i in range(SUBS):
-        rs = a_rows[i]
-        x2p[:, rs] += dot(z1t[:, last_own], a_v[rs, last_own], NT) + dot(z1t[:, last_peer], a_v[rs, last_peer], NT)
-        if i < 2:
-            for j in range(2 * i, 2 * i + 2):
-                x2_y.append(rcopy(x2p.at[:, ds(other0 + j * sub, sub)], x2_in.at[:, pl.ds(j * sub, sub)], X2Y_R + j, yn))
-                x2_y[-1].start()
+    for j in range(SUBS):
+        rs = ds(other0 + j * sub, sub)
+        more = part_x2(rs, peer_cols, 1)
+        if j >= 2:
+            more = more + part_x2(rs, my_cols, 1)
+        x2p[:, rs] += more
+        x2_y.append(rcopy(x2p.at[:, rs], x2_in.at[:, pl.ds(j * sub, sub)], X2Y_R + j, yn))
+        x2_y[-1].start()
+    for rs in a_rows[2:]:
+        x2p[:, rs] = dot(z1t[...], a_v[rs, :], NT)
 
     dw1 = None
     for i in range(SUBS):
@@ -265,7 +329,8 @@
     for copy in two_b:
         copy.start()
     one_d.wait_recv()
-    dw1_out[...] = one_tot[pl.ds(0, feat_in)]
+    dw1_store = pltpu.make_async_copy(one_tot, dw1_out, l_sem.at[6])
+    dw1_store.start()
     for copy in two_b:
         copy.wait_recv()
     two_mine = ds(c * n_two, n_two, 8)
@@ -273,7 +338,8 @@
     two_c = rcopy(two_tot.at[two_mine], two_tot.at[two_mine], TWO_R + 4, peer)
     two_c.start()
     two_c.wait_recv()
-    dw2t_out[...] = two_tot[pl.ds(0, classes)]
+    dw2_store = pltpu.make_async_copy(two_tot, dw2t_out, l_sem.at[7])
+    dw2_store.start()
 
     for copy in sent:
         copy.wait_send()
@@ -282,6 +348,8 @@
     def _():
         for copy in sent_off:
             copy.wait_send()
+    dw1_store.wait()
+    dw2_store.wait()
 
 
 def solution(mesh):
@@ -295,9 +363,9 @@
         one_half = vmem((fpad // 2, hidden), F32)
         dw1, dw2t = pl.pallas_call(
             gcn_kernel,
-            out_shape=(jax.ShapeDtypeStruct((feat_in, hidden), F32), jax.ShapeDtypeStruct((classes, hidden), F32)),
+            out_shape=(jax.ShapeDtypeStruct((fpad, hidden), F32), jax.ShapeDtypeStruct((cpad, hidden), F32)),
             in_specs=[pl.BlockSpec(memory_space=pltpu.HBM)] * 5,
-            out_specs=(pl.BlockSpec(memory_space=vmem), pl.BlockSpec(memory_space=vmem)),
+            out_specs=(pl.BlockSpec(memory_space=pltpu.HBM), pl.BlockSpec(memory_space=pltpu.HBM)),
             scratch_shapes=[
                 vmem((rows, cols), BF16),
                 vmem((feat_in, cols), BF16),
@@ -325,15 +393,15 @@
                 vmem((cpad // 2, hidden), F32),
                 vmem((4, cpad // 2, hidden), F32),
                 vmem((cpad, hidden), F32),
-                pltpu.SemaphoreType.DMA((4,)),
-                pltpu.SemaphoreType.DMA((5,)),
+                pltpu.SemaphoreType.DMA((8,)),
+                pltpu.SemaphoreType.DMA((8,)),
                 pltpu.SemaphoreType.DMA((N_SEND,)),
                 pltpu.SemaphoreType.DMA((N_RECV,)),
             ],
             compiler_params=pltpu.CompilerParams(
                 collective_id=0, has_side_effects=True, vmem_limit_bytes=60 * 1024 * 1024),
         )(adj, feat.T, w_one, w_two.T, grad.T)
-        return dw1, dw2t.T
+        return dw1[:feat_in], dw2t[:classes].T
 
     return jax.shard_map(
         local_step, mesh=mesh,

time: 69.1 us -> 65.8 us (0.952)
  Pallas kernels: 65.3 us -> 61.9 us
    pallas_call x1, Pallas kernels: 65.3 us -> 61.9 us  [local_step(): pl.pallas_call(gcn_kernel, out_shape=(jax.ShapeDtypeStruct((fpad, hidden)...]
    unnamed x2 -> x0, local copies, waits for them, and re-layouts: 2.97 us -> none
    slice x0 -> x1, local copies, waits for them, and re-layouts: none -> 1.55 us  [local_step(): return (dw1[:feat_in], dw2t[:classes].T)]
    transpose x0 -> x1, local copies, waits for them, and re-layouts: none -> 1.42 us  [local_step(): return (dw1[:feat_in], dw2t[:classes].T)]
where the time goes in v3:
time: 65.8 us; the launch traced here: 65.5 us
  Pallas kernels  61.9 us (94%)
  local copies, waits for them, and re-layouts  2.97 us (5%)
    pallas_call x1, Pallas kernels, local_step(): pl.pallas_call(gcn_kernel, out_shape=(jax.ShapeDtypeStruct((fpad, hidden)...  61.9 us
    slice x1, local copies, waits for them, and re-layouts, local_step(): return (dw1[:feat_in], dw2t[:classes].T)  1.55 us
    transpose x1, local copies, waits for them, and re-layouts, local_step(): return (dw1[:feat_in], dw2t[:classes].T)  1.42 us

profile of v3, /device:TPU:0, one launch (start us, length us, event | category | flops | bytes accessed | tf_op | source)
XLA Modules:
  0.0 65.5 jit_solution(1340074818897984451)
XLA Ops:
  0.6 61.9 %shard_map.68 = (f32[112,256]{1,0:T(8,128)}, f32[48,256]{1,0:T(8,128)}) custom-call(bf16[2048,4096]{1,0:T(8,128)(2,1)} %adj.1, bf16[100,2048]{1,0:T(8,128)(2,1)} %bitcast.5, bf16[100,256]{1,0:T(8,128)(2,1)} %w_one.1, bf16[47,256]{1,0:T(8,128)(2,1)} %bitcast.7, f32[47,2048]{1,0:T(8,128)} %bitcast.6), custom_call_target="tpu_custom_call" | custom-call | tf_op jit(solution)/shard_map/pallas_call | solution.py:364
  62.6 1.5 %slice.6 = f32[100,256]{1,0:T(8,128)} slice(f32[112,256]{1,0:T(8,128)} %get-tuple-element.4), slice={[0:100], [0:256]} | slice | bytes 204800 | tf_op jit(solution)/shard_map/slice | solution.py:404
  64.1 1.4 %slice_bitcast_fusion = f32[256,47]{0,1:T(8,128)} fusion(f32[48,256]{1,0:T(8,128)} %get-tuple-element.5), kind=kLoop, calls=%fused_computation | loop fusion | bytes 96256 | tf_op jit(solution)/shard_map/transpose | solution.py:404

commit v4 on v3

--- a/solution.py
+++ b/solution.py
@@ -1,5 +1,3 @@
-import itertools
-
 import jax
 import jax.numpy as jnp
 from jax import lax
@@ -14,8 +12,8 @@
 NT = (((1,), (1,)), ((), ()))
 TN = (((0,), (0,)), ((), ()))
 SUBS = 4
-N_SEND = 64
-H_R, HT_R, X1Y_R, X1G_R, X1D_R, DZD_R, DZX_R, X2Y_R, ONE_R, TWO_R, N_RECV = 0, 4, 8, 12, 20, 28, 30, 34, 38, 42, 47
+H_S, HT_S, X1Y_S, X1U_S, X1C_S, X1D_S, DZD_S, DZX_S, X2Y_S, ONE_S, TWO_S, N_SEND = 0, 1, 2, 3, 4, 5, 6, 7, 8, 9, 13, 16
+H_R, HT_R, X1Y_R, X1G_R, X1D_R, DZD_R, DZX_R, X2Y_R, ONE_R, TWO_R, N_RECV = 0, 2, 4, 8, 16, 20, 21, 23, 25, 29, 32
 
 
 def dot(lhs, rhs, dims):
@@ -48,20 +46,17 @@
     sub = half // SUBS
     feat_in, classes = feat.shape[0], grad.shape[0]
     my_cols, peer_cols = c * rows, (1 - c) * rows
-    send_ids = itertools.count()
-    sent, sent_diag, sent_off = [], [], []
-
-    def rcopy(src, dst, recv, dev, group=sent):
-        copy = pltpu.make_async_remote_copy(
-            src_ref=src, dst_ref=dst, send_sem=send_sem.at[next(send_ids)], recv_sem=recv_sem.at[recv],
+
+    def rcopy(src, dst, send, recv, dev):
+        return pltpu.make_async_remote_copy(
+            src_ref=src, dst_ref=dst, send_sem=send_sem.at[send], recv_sem=recv_sem.at[recv],
             device_id=dev, device_id_type=MESH)
-        group.append(copy)
-        return copy
 
     def wait_recv(dst, recv):
-        pltpu.make_async_remote_copy(
-            src_ref=dst, dst_ref=dst, send_sem=send_sem.at[0], recv_sem=recv_sem.at[recv],
-            device_id=peer, device_id_type=MESH).wait_recv()
+        rcopy(dst, dst, 0, recv, peer).wait_recv()
+
+    def wait_send(src, send):
+        rcopy(src, src, send, 0, peer).wait_send()
 
     side = jnp.where(diag, 0, 1)
     hs_loads = [pltpu.make_async_copy(feat.at[:, ds((2 * w + side) * quarter, quarter)],
@@ -83,13 +78,12 @@
     for i, start in enumerate((other0, other0 + quarter, own0, own0 + quarter)):
         for j in range(2):
             rs = ds(start + j * sub, sub)
-            a_loads.append(pltpu.make_async_copy(adj.at[rs], a_v.at[rs], a_sem.at[2 * i + j]))
+            a_loads.append(pltpu.make_async_copy(adj.at[rs], a_v.at[rs], a_sem.at[i]))
     for load in a_loads[:4]:
         load.start()
 
     def wait_a(i):
-        a_loads[2 * i].wait()
-        a_loads[2 * i + 1].wait()
+        pltpu.make_async_copy(adj.at[a_rows[i]], a_v.at[a_rows[i]], a_sem.at[i]).wait()
 
     barrier = pltpu.get_barrier_semaphore()
     for dev in (peer, xn, yn, opp):
@@ -101,19 +95,22 @@
 
     for w in range(2):
         hs_loads[w].wait()
-        rcopy(hs.at[:, pl.ds(w * quarter, quarter)], h_piece(2 * w + side), H_R + 2 * w + side, user).start()
+        rcopy(hs.at[:, pl.ds(w * quarter, quarter)], h_piece(2 * w + side), H_S, H_R + w, user).start()
 
     for load in a_loads[4:]:
         load.start()
     for load in (g_load, w1_load, w2_load):
         load.start()
-    h_fwd = [rcopy(h_piece(k), h_piece(k), HT_R + k, peer) for k in range(4)]
+    def h_wave(w, start):
+        return ht.at[:, ds(start + w * half, half)]
+
+    h_fwd = [rcopy(h_wave(w, my_cols), h_wave(w, my_cols), HT_S, HT_R + w, peer) for w in range(2)]
 
     @pl.when(diag)
     def _():
         h_load.wait()
-        for k in range(4):
-            h_fwd[k].start()
+        for w in range(2):
+            h_fwd[w].start()
 
     x1_y = []
 
@@ -122,7 +119,7 @@
         x1p[:, a_rows[i]] = part if first else x1p[:, a_rows[i]] + part
 
     for j in range(SUBS):
-        x1_y.append(rcopy(x1p.at[:, ds(other0 + j * sub, sub)], x1_in.at[:, pl.ds(j * sub, sub)], X1Y_R + j, yn))
+        x1_y.append(rcopy(x1p.at[:, ds(other0 + j * sub, sub)], x1_in.at[:, pl.ds(j * sub, sub)], X1Y_S, X1Y_R + j, yn))
 
     def send_x1(i, role):
         @pl.when(role)
@@ -133,23 +130,20 @@
     def forward_h(w):
         @pl.when(off)
         def _():
-            for k in (2 * w, 2 * w + 1):
-                wait_recv(h_piece(k), H_R + k)
-                h_fwd[k].start()
+            wait_recv(h_wave(w, my_cols), H_R + w)
+            h_fwd[w].start()
 
     waves = [(ds(my_cols + w * half, half), ds(peer_cols + w * half, half)) for w in range(2)]
     forward_h(0)
     for i in range(2):
         wait_a(i)
         add_x1(i, waves[0][0], True)
-    for k in range(2):
-        h_fwd[k].wait_recv()
+    h_fwd[0].wait_recv()
     for i in range(2):
         add_x1(i, waves[0][1])
     forward_h(1)
     add_x1(0, waves[1][0])
-    for k in range(2, 4):
-        h_fwd[k].wait_recv()
+    h_fwd[1].wait_recv()
     add_x1(0, waves[1][1])
     send_x1(0, off)
     add_x1(1, waves[1][0])
@@ -170,14 +164,14 @@
     def mine(ref, h, i):
         return ref.at[:, ds(my_cols + h * half + i * sub, sub)]
 
-    x1_fwd = {(h, i): rcopy(mine(x1t, hv, i), mine(x1t, hv, i), X1D_R + 4 * h + i, peer)
+    x1_fwd = {(h, i): rcopy(mine(x1t, hv, i), mine(x1t, hv, i), X1D_S, X1D_R + i, peer)
               for h, hv in ((0, y), (1, 1 - y)) for i in range(SUBS)}
     x1_user, x1_col = [], []
 
     for i in range(SUBS):
         piece = x1s.at[:, pl.ds(i * sub, sub)]
-        x1_user.append(rcopy(piece, mine(x1t, y, i), X1G_R + 4 * y + i, user))
-        x1_col.append(rcopy(piece, mine(x1t, y, i), X1G_R + 4 * y + i, yn, sent_off))
+        x1_user.append(rcopy(piece, mine(x1t, y, i), X1U_S, X1G_R + 4 * y + i, user))
+        x1_col.append(rcopy(piece, mine(x1t, y, i), X1C_S, X1G_R + 4 * y + i, yn))
 
     def sum_x1(i):
         x1_y[i].wait_recv()
@@ -202,20 +196,19 @@
 
     for i in range(2):
         backward(peer_cols + i * half)
-        dz_d2d.append(rcopy(dzp.at[:, ds(peer_cols + i * half, half)], dz_in.at[:, pl.ds(i * half, half)], DZD_R + i, peer))
+        dz_d2d.append(rcopy(dzp.at[:, ds(peer_cols + i * half, half)], dz_in.at[:, pl.ds(i * half, half)], DZD_S, DZD_R, peer))
         dz_d2d[-1].start()
         sum_x1(i)
     backward(my_cols)
     sum_x1(2)
     backward(my_cols + half)
-    for copy in dz_d2d:
-        copy.wait_recv()
+    wait_recv(dz_in, DZD_R)
     dz_s[...] = dzp[:, ds(my_cols + (1 - x) * half, half)] + dz_in[:, ds((1 - x) * half, half)]
     sum_x1(3)
     dz_x_copies = []
     for i in range(SUBS):
         cs = pl.ds(i * sub, sub)
-        dz_x_copies.append(rcopy(dz_s.at[:, cs], dz_x.at[:, cs], DZX_R + i, xn))
+        dz_x_copies.append(rcopy(dz_s.at[:, cs], dz_x.at[:, cs], DZX_S, DZX_R + i // (SUBS - 1), xn))
 
     def send_dz(role):
         @pl.when(role)
@@ -244,8 +237,7 @@
             hidden(my_cols + h + i * sub, sub)
 
     def peer_piece(i):
-        x1_fwd[0, i].wait_recv()
-        x1_fwd[1, i].wait_recv()
+        wait_recv(x1t.at[:, pl.ds(0, 2 * sub)], X1D_R + i)
         for h in halves:
             hidden(peer_cols + h + i * sub, sub)
 
@@ -276,14 +268,17 @@
         if j >= 2:
             more = more + part_x2(rs, my_cols, 1)
         x2p[:, rs] += more
-        x2_y.append(rcopy(x2p.at[:, rs], x2_in.at[:, pl.ds(j * sub, sub)], X2Y_R + j, yn))
+        x2_y.append(rcopy(x2p.at[:, rs], x2_in.at[:, pl.ds(j * sub, sub)], X2Y_S, X2Y_R + j // (SUBS - 1), yn))
         x2_y[-1].start()
     for rs in a_rows[2:]:
         x2p[:, rs] = dot(z1t[...], a_v[rs, :], NT)
 
     dw1 = None
     for i in range(SUBS):
-        dz_x_copies[i].wait_recv()
+        if i == 0:
+            wait_recv(dz_x.at[:, pl.ds(0, half - sub)], DZX_R)
+        if i == SUBS - 1:
+            wait_recv(dz_x.at[:, pl.ds(0, sub)], DZX_R + 1)
         cs = ds(my_cols + x * half + i * sub, sub)
         d_hidden = (dzp[:, cs] + dz_in[:, ds(x * half + i * sub, sub)]) + dz_x[:, pl.ds(i * sub, sub)]
         d_pre = jnp.where(z1t[:, cs].astype(F32) > 0.0, d_hidden, 0.0).astype(BF16)
@@ -293,20 +288,23 @@
     one_p[pl.ds(feat_in, one_p.shape[0] - feat_in)] = jnp.zeros((one_p.shape[0] - feat_in, one_p.shape[1]), F32)
 
     n_one = one_p.shape[0] // 2
-    one_a = rcopy(one_p.at[ds((1 - c) * n_one, n_one, 8)], one_in, ONE_R, peer)
+    one_a = rcopy(one_p.at[ds((1 - c) * n_one, n_one, 8)], one_in, ONE_S, ONE_R, peer)
     one_a.start()
     one_a.wait_recv()
     one_s[...] = one_p[ds(c * n_one, n_one, 8)] + one_in[...]
-    one_b = rcopy(one_s, one_x, ONE_R + 1, xn)
+    one_b = rcopy(one_s, one_x, ONE_S + 1, ONE_R + 1, xn)
     one_b.start()
     one_b.wait_recv()
     one_sx[...] = one_s[...] + one_x[...]
-    one_c = rcopy(one_sx, one_y, ONE_R + 2, yn)
+    one_c = rcopy(one_sx, one_y, ONE_S + 2, ONE_R + 2, yn)
     one_c.start()
 
     dw2 = None
     for i in range(SUBS):
-        x2_y[i].wait_recv()
+        if i == 0:
+            wait_recv(x2_in.at[:, pl.ds(0, half - sub)], X2Y_R)
+        if i == SUBS - 1:
+            wait_recv(x2_in.at[:, pl.ds(0, sub)], X2Y_R + 1)
         rs = ds(own0 + i * sub, sub)
         act = (x2p[:, rs] + x2_in[:, pl.ds(i * sub, sub)]).astype(BF16)
         part = dot(gbt[:, rs], act, NT)
@@ -316,40 +314,53 @@
 
     n_two = two_p.shape[0] // 2
     chip = 2 * x + y
-    two_a = rcopy(two_p.at[ds((1 - c) * n_two, n_two, 8)], two_in, TWO_R, peer)
+    two_a = rcopy(two_p.at[ds((1 - c) * n_two, n_two, 8)], two_in, TWO_S, TWO_R, peer)
     two_a.start()
     one_c.wait_recv()
     one_mine = ds(c * n_one, n_one, 8)
     one_tot[one_mine] = one_sx[...] + one_y[...]
-    one_d = rcopy(one_tot.at[one_mine], one_tot.at[one_mine], ONE_R + 3, peer)
+    one_d = rcopy(one_tot.at[one_mine], one_tot.at[one_mine], ONE_S + 3, ONE_R + 3, peer)
     one_d.start()
     two_a.wait_recv()
     two_all[chip] = two_p[ds(c * n_two, n_two, 8)] + two_in[...]
-    two_b = [rcopy(two_all.at[chip], two_all.at[chip], TWO_R + 1 + i, dev) for i, dev in enumerate((opp, xn, yn))]
+    two_b = [rcopy(two_all.at[chip], two_all.at[chip], TWO_S + 1, TWO_R + 1, dev) for dev in (opp, xn, yn)]
     for copy in two_b:
         copy.start()
     one_d.wait_recv()
     dw1_store = pltpu.make_async_copy(one_tot, dw1_out, l_sem.at[6])
     dw1_store.start()
-    for copy in two_b:
-        copy.wait_recv()
+    wait_recv(two_all.at[pl.ds(0, 3)], TWO_R + 1)
     two_mine = ds(c * n_two, n_two, 8)
     two_tot[two_mine] = (two_all[0] + two_all[1]) + (two_all[2] + two_all[3])
-    two_c = rcopy(two_tot.at[two_mine], two_tot.at[two_mine], TWO_R + 4, peer)
+    two_c = rcopy(two_tot.at[two_mine], two_tot.at[two_mine], TWO_S + 2, TWO_R + 2, peer)
     two_c.start()
     two_c.wait_recv()
     dw2_store = pltpu.make_async_copy(two_tot, dw2t_out, l_sem.at[7])
     dw2_store.start()
 
-    for copy in sent:
-        copy.wait_send()
+    wait_send(hs, H_S)
+    wait_send(ht.at[:, pl.ds(0, rows)], HT_S)
+    wait_send(x1_in, X1Y_S)
+    wait_send(x1s, X1U_S)
 
     @pl.when(off)
     def _():
-        for copy in sent_off:
-            copy.wait_send()
+        wait_send(x1s, X1C_S)
+
+    wait_send(x1t.at[:, pl.ds(0, rows)], X1D_S)
+    wait_send(dz_in, DZD_S)
+    wait_send(dz_s, DZX_S)
+    wait_send(x2_in, X2Y_S)
+    for copy in (one_a, one_b, one_c, one_d, two_a, two_c):
+        copy.wait_send()
+    wait_send(two_all.at[pl.ds(0, 3)], TWO_S + 1)
     dw1_store.wait()
     dw2_store.wait()
+
+
+def finish_kernel(one, two, dw1, dw2t):
+    dw1[...] = one[pl.ds(0, dw1.shape[0])]
+    dw2t[...] = two[pl.ds(0, dw2t.shape[0])]
 
 
 def solution(mesh):
@@ -393,7 +404,7 @@
                 vmem((cpad // 2, hidden), F32),
                 vmem((4, cpad // 2, hidden), F32),
                 vmem((cpad, hidden), F32),
-                pltpu.SemaphoreType.DMA((8,)),
+                pltpu.SemaphoreType.DMA((4,)),
                 pltpu.SemaphoreType.DMA((8,)),
                 pltpu.SemaphoreType.DMA((N_SEND,)),
                 pltpu.SemaphoreType.DMA((N_RECV,)),
@@ -401,7 +412,13 @@
             compiler_params=pltpu.CompilerParams(
                 collective_id=0, has_side_effects=True, vmem_limit_bytes=60 * 1024 * 1024),
         )(adj, feat.T, w_one, w_two.T, grad.T)
-        return dw1[:feat_in], dw2t[:classes].T
+        dw1, dw2t = pl.pallas_call(
+            finish_kernel,
+            out_shape=(jax.ShapeDtypeStruct((feat_in, hidden), F32), jax.ShapeDtypeStruct((classes, hidden), F32)),
+            in_specs=[pl.BlockSpec(memory_space=vmem)] * 2,
+            out_specs=(pl.BlockSpec(memory_space=vmem),) * 2,
+        )(dw1, dw2t)
+        return dw1, dw2t.T
 
     return jax.shard_map(
         local_step, mesh=mesh,

time: 65.8 us -> 63.7 us (0.968)
  local copies, waits for them, and re-layouts: 2.97 us -> 0 us
  Pallas kernels: 61.9 us -> 62.9 us
    pallas_call x0 -> x1, Pallas kernels: none -> 1.56 us  [local_step(): pl.pallas_call(finish_kernel, out_shape=(jax.ShapeDtypeStruct((feat_in, h...]
    slice x1 -> x0, local copies, waits for them, and re-layouts: 1.55 us -> none  [local_step(): return (dw1[:feat_in], dw2t[:classes].T)]
    transpose x1 -> x0, local copies, waits for them, and re-layouts: 1.42 us -> none  [local_step(): return (dw1[:feat_in], dw2t[:classes].T)]
where the time goes in v4:
time: 63.7 us; the launch traced here: 63.5 us
  Pallas kernels  62.9 us (99%)
  between operations  0.64 us (1%)
    pallas_call x1, Pallas kernels, local_step(): pl.pallas_call(gcn_kernel, out_shape=(jax.ShapeDtypeStruct((fpad, hidden)...  61.3 us
    pallas_call x1, Pallas kernels, local_step(): pl.pallas_call(finish_kernel, out_shape=(jax.ShapeDtypeStruct((feat_in, h...  1.56 us

profile of v4, /device:TPU:0, one launch (start us, length us, event | category | flops | bytes accessed | tf_op | source)
XLA Modules:
  0.0 63.5 jit_solution(12073056682622548888)
XLA Ops:
  0.6 61.3 %shard_map.68 = (f32[112,256]{1,0:T(8,128)}, f32[48,256]{1,0:T(8,128)}) custom-call(bf16[2048,4096]{1,0:T(8,128)(2,1)} %adj.1, bf16[100,2048]{1,0:T(8,128)(2,1)} %bitcast.4, bf16[100,256]{1,0:T(8,128)(2,1)} %w_one.1, bf16[47,256]{1,0:T(8,128)(2,1)} %bitcast.6, f32[47,2048]{1,0:T(8,128)} %bitcast.5), custom_call_target="tpu_custom_call" | custom-call | tf_op jit(solution)/shard_map/pallas_call | solution.py:375
  61.9 1.6 %shard_map.69 = (f32[100,256]{1,0:T(8,128)}, f32[47,256]{1,0:T(8,128)}) custom-call(f32[112,256]{1,0:T(8,128)} %get-tuple-element.6.one, f32[48,256]{1,0:T(8,128)} %get-tuple-element.7.two), custom_call_target="tpu_custom_call" | custom-call | tf_op jit(solution)/shard_map/pallas_call | solution.py:415

commit v5 on v4

--- a/solution.py
+++ b/solution.py
@@ -114,18 +114,18 @@
 
     x1_y = []
 
-    def add_x1(i, cs, first=False):
-        part = dot(ht[:, cs], a_v[a_rows[i], cs], NT)
-        x1p[:, a_rows[i]] = part if first else x1p[:, a_rows[i]] + part
+    def add_x1(rs, cs, first=False):
+        part = dot(ht[:, cs], a_v[rs, cs], NT)
+        x1p[:, rs] = part if first else x1p[:, rs] + part
 
     for j in range(SUBS):
         x1_y.append(rcopy(x1p.at[:, ds(other0 + j * sub, sub)], x1_in.at[:, pl.ds(j * sub, sub)], X1Y_S, X1Y_R + j, yn))
 
-    def send_x1(i, role):
+    def send_x1(subs, role):
         @pl.when(role)
         def _():
-            x1_y[2 * i].start()
-            x1_y[2 * i + 1].start()
+            for j in subs:
+                x1_y[j].start()
 
     def forward_h(w):
         @pl.when(off)
@@ -137,20 +137,20 @@
     forward_h(0)
     for i in range(2):
         wait_a(i)
-        add_x1(i, waves[0][0], True)
+        add_x1(a_rows[i], waves[0][0], True)
     h_fwd[0].wait_recv()
     for i in range(2):
-        add_x1(i, waves[0][1])
+        add_x1(a_rows[i], waves[0][1])
     forward_h(1)
-    add_x1(0, waves[1][0])
+    add_x1(a_rows[0], waves[1][0])
     h_fwd[1].wait_recv()
-    add_x1(0, waves[1][1])
-    send_x1(0, off)
-    add_x1(1, waves[1][0])
-    add_x1(1, waves[1][1])
-    send_x1(0, diag)
-    send_x1(1, diag)
-    send_x1(1, off)
+    for j in range(2):
+        add_x1(ds(other0 + j * sub, sub), waves[1][1])
+        send_x1((j,), off)
+    add_x1(a_rows[1], waves[1][0])
+    add_x1(a_rows[1], waves[1][1])
+    send_x1(range(SUBS), diag)
+    send_x1((2, 3), off)
     for i in range(2, 4):
         wait_a(i)
         x1p[:, a_rows[i]] = dot(ht[...], a_v[a_rows[i], :], NT)
@@ -256,7 +256,6 @@
     peer_piece(1)
     x2p[:, a_rows[0]] = part_x2(a_rows[0], my_cols, 0) + part_x2(a_rows[0], peer_cols, 0)
     own_piece(2)
-    x2p[:, a_rows[1]] = part_x2(a_rows[1], my_cols, 0) + part_x2(a_rows[1], peer_cols, 0)
     own_piece(3)
     peer_piece(2)
     x2p[:, a_rows[0]] += part_x2(a_rows[0], my_cols, 1)
@@ -264,10 +263,10 @@
     x2_y = []
     for j in range(SUBS):
         rs = ds(other0 + j * sub, sub)
-        more = part_x2(rs, peer_cols, 1)
-        if j >= 2:
-            more = more + part_x2(rs, my_cols, 1)
-        x2p[:, rs] += more
+        if j < 2:
+            x2p[:, rs] += part_x2(rs, peer_cols, 1)
+        if j == 2:
+            x2p[:, a_rows[1]] = dot(z1t[...], a_v[a_rows[1], :], NT)
         x2_y.append(rcopy(x2p.at[:, rs], x2_in.at[:, pl.ds(j * sub, sub)], X2Y_S, X2Y_R + j // (SUBS - 1), yn))
         x2_y[-1].start()
     for rs in a_rows[2:]:
@@ -316,16 +315,16 @@
     chip = 2 * x + y
     two_a = rcopy(two_p.at[ds((1 - c) * n_two, n_two, 8)], two_in, TWO_S, TWO_R, peer)
     two_a.start()
+    two_a.wait_recv()
+    two_all[chip] = two_p[ds(c * n_two, n_two, 8)] + two_in[...]
+    two_b = [rcopy(two_all.at[chip], two_all.at[chip], TWO_S + 1, TWO_R + 1, dev) for dev in (opp, xn, yn)]
+    for copy in two_b:
+        copy.start()
     one_c.wait_recv()
     one_mine = ds(c * n_one, n_one, 8)
     one_tot[one_mine] = one_sx[...] + one_y[...]
     one_d = rcopy(one_tot.at[one_mine], one_tot.at[one_mine], ONE_S + 3, ONE_R + 3, peer)
     one_d.start()
-    two_a.wait_recv()
-    two_all[chip] = two_p[ds(c * n_two, n_two, 8)] + two_in[...]
-    two_b = [rcopy(two_all.at[chip], two_all.at[chip], TWO_S + 1, TWO_R + 1, dev) for dev in (opp, xn, yn)]
-    for copy in two_b:
-        copy.start()
     one_d.wait_recv()
     dw1_store = pltpu.make_async_copy(one_tot, dw1_out, l_sem.at[6])
     dw1_store.start()

time: 63.7 us -> 62.9 us (0.987)
  Pallas kernels: 62.9 us -> 62.2 us
    pallas_call x1, Pallas kernels: 61.3 us -> 60.6 us  [local_step(): pl.pallas_call(gcn_kernel, out_shape=(jax.ShapeDtypeStruct((fpad, hidden)...]
where the time goes in v5:
time: 62.9 us; the launch traced here: 62.8 us
  Pallas kernels  62.2 us (99%)
  between operations  0.64 us (1%)
    pallas_call x1, Pallas kernels, local_step(): pl.pallas_call(gcn_kernel, out_shape=(jax.ShapeDtypeStruct((fpad, hidden)...  60.6 us
    pallas_call x1, Pallas kernels, local_step(): pl.pallas_call(finish_kernel, out_shape=(jax.ShapeDtypeStruct((feat_in, h...  1.56 us

profile of v5, /device:TPU:0, one launch (start us, length us, event | category | flops | bytes accessed | tf_op | source)
XLA Modules:
  0.0 62.8 jit_solution(10460016209194535579)
XLA Ops:
  0.6 60.6 %shard_map.68 = (f32[112,256]{1,0:T(8,128)}, f32[48,256]{1,0:T(8,128)}) custom-call(bf16[2048,4096]{1,0:T(8,128)(2,1)} %adj.1, bf16[100,2048]{1,0:T(8,128)(2,1)} %bitcast.4, bf16[100,256]{1,0:T(8,128)(2,1)} %w_one.1, bf16[47,256]{1,0:T(8,128)(2,1)} %bitcast.6, f32[47,2048]{1,0:T(8,128)} %bitcast.5), custom_call_target="tpu_custom_call" | custom-call | tf_op jit(solution)/shard_map/pallas_call | solution.py:374
  61.2 1.6 %shard_map.69 = (f32[100,256]{1,0:T(8,128)}, f32[47,256]{1,0:T(8,128)}) custom-call(f32[112,256]{1,0:T(8,128)} %get-tuple-element.6.one, f32[48,256]{1,0:T(8,128)} %get-tuple-element.7.two), custom_call_target="tpu_custom_call" | custom-call | tf_op jit(solution)/shard_map/pallas_call | solution.py:414

commit v6 on v5

--- a/solution.py
+++ b/solution.py
@@ -12,8 +12,8 @@
 NT = (((1,), (1,)), ((), ()))
 TN = (((0,), (0,)), ((), ()))
 SUBS = 4
-H_S, HT_S, X1Y_S, X1U_S, X1C_S, X1D_S, DZD_S, DZX_S, X2Y_S, ONE_S, TWO_S, N_SEND = 0, 1, 2, 3, 4, 5, 6, 7, 8, 9, 13, 16
-H_R, HT_R, X1Y_R, X1G_R, X1D_R, DZD_R, DZX_R, X2Y_R, ONE_R, TWO_R, N_RECV = 0, 2, 4, 8, 16, 20, 21, 23, 25, 29, 32
+H_S, HT_S, X1Y_S, X1U_S, X1C_S, X1D_S, DZD_S, DZX_S, X2Y_S, ONE_S, TWO_S, N_SEND = 0, 1, 2, 3, 4, 5, 6, 7, 8, 9, 13, 15
+H_R, HT_R, X1Y_R, X1G_R, X1D_R, DZD_R, DZX_R, X2Y_R, ONE_R, TWO_R, N_RECV = 0, 2, 4, 8, 16, 20, 21, 23, 25, 29, 31
 
 
 def dot(lhs, rhs, dims):
@@ -28,7 +28,7 @@
     adj, feat, w_one, w_two, grad, dw1_out, dw2t_out,
     a_v, ht, hs, g_v, w1_v, w2_v, gbt, dyt, dzp, dz_in, dz_s, dz_x,
     x1p, x1_in, x1s, x1t, z1t, x2p, x2_in,
-    one_p, one_in, one_s, one_x, one_sx, one_y, one_tot, two_p, two_in, two_all, two_tot,
+    one_p, one_in, one_s, one_x, one_sx, one_y, one_tot, two_p, two_all, two_tot,
     a_sem, l_sem, send_sem, recv_sem,
 ):
     y = lax.axis_index("rep")
@@ -40,6 +40,7 @@
     xn = (y, 2 * (1 - x) + c)
     yn = (1 - y, r)
     opp = (1 - y, 2 * (1 - x) + c)
+    far = [(yy, 2 * xx + cc) for yy, xx in ((1 - y, 1 - x), (y, 1 - x), (1 - y, x)) for cc in (c, 1 - c)]
     user = (x, 2 * (1 - x) + c)
     rows, cols = a_v.shape
     half, quarter = rows // 2, rows // 4
@@ -86,9 +87,9 @@
         pltpu.make_async_copy(adj.at[a_rows[i]], a_v.at[a_rows[i]], a_sem.at[i]).wait()
 
     barrier = pltpu.get_barrier_semaphore()
-    for dev in (peer, xn, yn, opp):
+    for dev in (peer, *far):
         pl.semaphore_signal(barrier, inc=1, device_id=dev, device_id_type=MESH)
-    pl.semaphore_wait(barrier, 4)
+    pl.semaphore_wait(barrier, 7)
 
     def h_piece(k):
         return ht.at[:, ds(my_cols + k * quarter, quarter)]
@@ -250,8 +251,8 @@
         return total
 
     own_piece(0)
+    own_piece(1)
     send_dz(diag)
-    own_piece(1)
     peer_piece(0)
     peer_piece(1)
     x2p[:, a_rows[0]] = part_x2(a_rows[0], my_cols, 0) + part_x2(a_rows[0], peer_cols, 0)
@@ -293,10 +294,16 @@
     one_s[...] = one_p[ds(c * n_one, n_one, 8)] + one_in[...]
     one_b = rcopy(one_s, one_x, ONE_S + 1, ONE_R + 1, xn)
     one_b.start()
-    one_b.wait_recv()
-    one_sx[...] = one_s[...] + one_x[...]
     one_c = rcopy(one_sx, one_y, ONE_S + 2, ONE_R + 2, yn)
-    one_c.start()
+
+    def send_one_y(role):
+        @pl.when(role)
+        def _():
+            one_b.wait_recv()
+            one_sx[...] = one_s[...] + one_x[...]
+            one_c.start()
+
+    send_one_y(off)
 
     dw2 = None
     for i in range(SUBS):
@@ -312,27 +319,26 @@
     two_p[pl.ds(classes, two_p.shape[0] - classes)] = jnp.zeros((two_p.shape[0] - classes, two_p.shape[1]), F32)
 
     n_two = two_p.shape[0] // 2
-    chip = 2 * x + y
-    two_a = rcopy(two_p.at[ds((1 - c) * n_two, n_two, 8)], two_in, TWO_S, TWO_R, peer)
-    two_a.start()
-    two_a.wait_recv()
-    two_all[chip] = two_p[ds(c * n_two, n_two, 8)] + two_in[...]
-    two_b = [rcopy(two_all.at[chip], two_all.at[chip], TWO_S + 1, TWO_R + 1, dev) for dev in (opp, xn, yn)]
-    for copy in two_b:
-        copy.start()
+    me = 2 * (2 * x + y) + c
+    two_mine, two_peer = ds(c * n_two, n_two, 8), ds((1 - c) * n_two, n_two, 8)
+    for k, dev in enumerate((*far, peer)):
+        rows_k = two_mine if k < 6 and k % 2 == 0 else two_peer
+        rcopy(two_p.at[rows_k], two_all.at[me], TWO_S, TWO_R, dev).start()
+    two_all[me] = two_p[two_mine]
+    send_one_y(diag)
     one_c.wait_recv()
     one_mine = ds(c * n_one, n_one, 8)
     one_tot[one_mine] = one_sx[...] + one_y[...]
     one_d = rcopy(one_tot.at[one_mine], one_tot.at[one_mine], ONE_S + 3, ONE_R + 3, peer)
     one_d.start()
+    wait_recv(two_all.at[pl.ds(0, 7)], TWO_R)
+    pairs = [two_all[2 * k] + two_all[2 * k + 1] for k in range(4)]
+    two_tot[two_mine] = (pairs[0] + pairs[1]) + (pairs[2] + pairs[3])
+    two_c = rcopy(two_tot.at[two_mine], two_tot.at[two_mine], TWO_S + 1, TWO_R + 1, peer)
+    two_c.start()
     one_d.wait_recv()
     dw1_store = pltpu.make_async_copy(one_tot, dw1_out, l_sem.at[6])
     dw1_store.start()
-    wait_recv(two_all.at[pl.ds(0, 3)], TWO_R + 1)
-    two_mine = ds(c * n_two, n_two, 8)
-    two_tot[two_mine] = (two_all[0] + two_all[1]) + (two_all[2] + two_all[3])
-    two_c = rcopy(two_tot.at[two_mine], two_tot.at[two_mine], TWO_S + 2, TWO_R + 2, peer)
-    two_c.start()
     two_c.wait_recv()
     dw2_store = pltpu.make_async_copy(two_tot, dw2t_out, l_sem.at[7])
     dw2_store.start()
@@ -350,9 +356,9 @@
     wait_send(dz_in, DZD_S)
     wait_send(dz_s, DZX_S)
     wait_send(x2_in, X2Y_S)
-    for copy in (one_a, one_b, one_c, one_d, two_a, two_c):
+    for copy in (one_a, one_b, one_c, one_d, two_c):
         copy.wait_send()
-    wait_send(two_all.at[pl.ds(0, 3)], TWO_S + 1)
+    wait_send(two_all.at[pl.ds(0, 7)], TWO_S)
     dw1_store.wait()
     dw2_store.wait()
 
@@ -400,8 +406,7 @@
                 *[one_half] * 5,
                 vmem((fpad, hidden), F32),
                 vmem((cpad, hidden), F32),
-                vmem((cpad // 2, hidden), F32),
-                vmem((4, cpad // 2, hidden), F32),
+                vmem((8, cpad // 2, hidden), F32),
                 vmem((cpad, hidden), F32),
                 pltpu.SemaphoreType.DMA((4,)),
                 pltpu.SemaphoreType.DMA((8,)),

time: 62.9 us -> 62.6 us (level)
  no operation moved by 1% of the time
where the time goes in v6:
time: 62.6 us; the launch traced here: 62.5 us
  Pallas kernels  61.8 us (99%)
  between operations  0.64 us (1%)
    pallas_call x1, Pallas kernels, local_step(): pl.pallas_call(gcn_kernel, out_shape=(jax.ShapeDtypeStruct((fpad, hidden)...  60.3 us
    pallas_call x1, Pallas kernels, local_step(): pl.pallas_call(finish_kernel, out_shape=(jax.ShapeDtypeStruct((feat_in, h...  1.56 us

profile of v6, /device:TPU:0, one launch (start us, length us, event | category | flops | bytes accessed | tf_op | source)
XLA Modules:
  0.0 62.5 jit_solution(2638154201763738707)
XLA Ops:
  0.6 60.3 %shard_map.68 = (f32[112,256]{1,0:T(8,128)}, f32[48,256]{1,0:T(8,128)}) custom-call(bf16[2048,4096]{1,0:T(8,128)(2,1)} %adj.1, bf16[100,2048]{1,0:T(8,128)(2,1)} %bitcast.4, bf16[100,256]{1,0:T(8,128)(2,1)} %w_one.1, bf16[47,256]{1,0:T(8,128)(2,1)} %bitcast.6, f32[47,2048]{1,0:T(8,128)} %bitcast.5), custom_call_target="tpu_custom_call" | custom-call | tf_op jit(solution)/shard_map/pallas_call | solution.py:380
  60.9 1.6 %shard_map.69 = (f32[100,256]{1,0:T(8,128)}, f32[47,256]{1,0:T(8,128)}) custom-call(f32[112,256]{1,0:T(8,128)} %get-tuple-element.6.one, f32[48,256]{1,0:T(8,128)} %get-tuple-element.7.two), custom_call_target="tpu_custom_call" | custom-call | tf_op jit(solution)/shard_map/pallas_call | solution.py:419

commit v7 on v6

--- a/solution.py
+++ b/solution.py
@@ -135,6 +135,15 @@
             h_fwd[w].start()
 
     waves = [(ds(my_cols + w * half, half), ds(peer_cols + w * half, half)) for w in range(2)]
+    def make_dy(role):
+        @pl.when(role)
+        def _():
+            g_load.wait()
+            w2_load.wait()
+            gbt[...] = g_v[...].astype(BF16)
+            dyt[...] = dot(w2_v[...], gbt[...], TN).astype(BF16)
+
+    make_dy(off)
     forward_h(0)
     for i in range(2):
         wait_a(i)
@@ -190,11 +199,7 @@
         def _():
             x1_col[i].start()
 
-    g_load.wait()
-    w2_load.wait()
-    gbt[...] = g_v[...].astype(BF16)
-    dyt[...] = dot(w2_v[...], gbt[...], TN).astype(BF16)
-
+    make_dy(diag)
     for i in range(2):
         backward(peer_cols + i * half)
         dz_d2d.append(rcopy(dzp.at[:, ds(peer_cols + i * half, half)], dz_in.at[:, pl.ds(i * half, half)], DZD_S, DZD_R, peer))

time: 62.6 us -> 62.6 us (level)
  no operation moved by 1% of the time
where the time goes in v7:
time: 62.6 us; the launch traced here: 62.5 us
  Pallas kernels  61.8 us (99%)
  between operations  0.64 us (1%)
    pallas_call x1, Pallas kernels, local_step(): pl.pallas_call(gcn_kernel, out_shape=(jax.ShapeDtypeStruct((fpad, hidden)...  60.3 us
    pallas_call x1, Pallas kernels, local_step(): pl.pallas_call(finish_kernel, out_shape=(jax.ShapeDtypeStruct((feat_in, h...  1.56 us

profile of v7, /device:TPU:0, one launch (start us, length us, event | category | flops | bytes accessed | tf_op | source)
XLA Modules:
  0.0 62.5 jit_solution(221024672266422850)
XLA Ops:
  0.6 60.3 %shard_map.68 = (f32[112,256]{1,0:T(8,128)}, f32[48,256]{1,0:T(8,128)}) custom-call(bf16[2048,4096]{1,0:T(8,128)(2,1)} %adj.1, bf16[100,2048]{1,0:T(8,128)(2,1)} %bitcast.4, bf16[100,256]{1,0:T(8,128)(2,1)} %w_one.1, bf16[47,256]{1,0:T(8,128)(2,1)} %bitcast.6, f32[47,2048]{1,0:T(8,128)} %bitcast.5), custom_call_target="tpu_custom_call" | custom-call | tf_op jit(solution)/shard_map/pallas_call | solution.py:385
  60.9 1.6 %shard_map.69 = (f32[100,256]{1,0:T(8,128)}, f32[47,256]{1,0:T(8,128)}) custom-call(f32[112,256]{1,0:T(8,128)} %get-tuple-element.6.one, f32[48,256]{1,0:T(8,128)} %get-tuple-element.7.two), custom_call_target="tpu_custom_call" | custom-call | tf_op jit(solution)/shard_map/pallas_call | solution.py:424
